TPU v7x, 128 devices: a whole 4x4x4 slice. The times are simulated.
128 devices in a mesh: row: 8 (over z, x_hi), col: 16 (over y, x_lo, core).
Axes of the slice: x: 4 (x_hi: 2, x_lo: 2; x = x_hi * 2 + x_lo), y: 4, z: 4, core: 2. Of those that a mesh axis runs over, the one named last changes fastest.
Arguments:
- diag_blocks: float32 [16, 32, 512, 512], P('row', 'col'), may hold values from -4 to 16, as said below
- horizontal: bfloat16 [16, 32, 512, 512], P('row', 'col'), may hold values from -0.125 to 0.125
- vertical: bfloat16 [16, 32, 512, 512], P('row', 'col'), may hold values from -0.125 to 0.125
Outputs:
- red_factor: float32 [16, 16, 512, 512], P('row', 'col')
- black_schur: float32 [16, 16, 512, 512], P('row', 'col')
- black_links: bfloat16 [16, 16, 4, 512, 512], P('row', 'col')
Inputs may be any that keep to these rules, and one draw needn't show every extreme that they name: `diag_blocks`: every block is symmetric and its eigenvalues are at least 1.
All inputs are finite; a program needn't handle non-finite values.
Results may differ from a plain program's by a relative error of at most 0.0054.
Values may be sent and summed in bfloat16 or wider, within the bound.
A program may use at most 128 MiB of HBM per device.

v0:
```python
import jax
import jax.numpy as jnp
from jax import lax
from jax.experimental import pallas as pl
from jax.experimental.pallas import tpu as pltpu
from jax.sharding import PartitionSpec as P

N = 512
NB = 128
SB = 16
F32 = jnp.float32
BF16 = jnp.bfloat16


def dot(a, b, ca=1, cb=0):
    return lax.dot_general(a, b, (((ca,), (cb,)), ((), ())), preferred_element_type=F32)


def split(x):
    hi = x.astype(BF16)
    return hi, (x - hi.astype(F32)).astype(BF16)


def dot3(a, b, cb=0):
    ah, al = a
    bh, bl = b
    if cb == 1:
        return dot(ah, bh, 1, 1) + dot(al, bh, 1, 1) + dot(ah, bl, 1, 1)
    return dot(jnp.concatenate([ah, al], 1), jnp.concatenate([bh, bh], 0)) + dot(ah, bl)


def rows8(x, k):
    return jnp.broadcast_to(x[k : k + 1, :], (8, NB))


def eliminate(s, x_ref, p_ref, s_ref):
    k0 = SB * s
    row = lax.broadcasted_iota(jnp.int32, (8, NB), 0)
    xs = [[x_ref[k0 + 8 * h : k0 + 8 * h + 8, NB * w : NB * w + NB] for h in range(2)] for w in range(2)]
    cols = [
        [jnp.broadcast_to(xs[0][h][:, k0 + c : k0 + c + 1], (8, NB)) for h in range(2)]
        for c in range(SB)
    ]
    pivots = [jnp.ones((8, NB), F32) for _ in range(2)]
    saved = [[xs[w][h] for h in range(2)] for w in range(2)]
    for k in range(SB):
        kh, kr = divmod(k, 8)
        is_k = row == kr
        pivot = rows8(cols[k][kh], kr)
        inverse = 1.0 / pivot
        mult = [cols[k][h] * inverse for h in range(2)]
        mult[kh] = jnp.where(is_k, 0.0, mult[kh])
        for c in range(k + 1, SB):
            head = rows8(cols[c][kh], kr)
            cols[c] = [cols[c][h] - mult[h] * head for h in range(2)]
        pivots[kh] = jnp.where(is_k, pivot, pivots[kh])
        for w in range(2):
            saved[w][kh] = jnp.where(is_k, xs[w][kh], saved[w][kh])
            head = rows8(xs[w][kh], kr)
            xs[w] = [xs[w][h] - mult[h] * head for h in range(2)]
    for h in range(2):
        scale = lax.rsqrt(pivots[h])
        s_ref[k0 + 8 * h : k0 + 8 * h + 8, 0:NB] = scale
        s_ref[k0 + 8 * h : k0 + 8 * h + 8, NB : 2 * NB] = pivots[h] * scale
        for w in range(2):
            p_ref[k0 + 8 * h : k0 + 8 * h + 8, NB * w : NB * w + NB] = saved[w][h] * scale
    below = NB - k0 - SB
    if below:
        z = jnp.concatenate(
            [jnp.concatenate([xs[w][h] / pivots[h] for w in range(2)], 1) for h in range(2)], 0
        )
        zh, zl = split(z)

        def pad(v):
            parts = [v]
            if k0:
                parts.insert(0, jnp.zeros((k0, 2 * NB), BF16))
            parts.append(jnp.zeros((below, 2 * NB), BF16))
            return jnp.concatenate(parts, 0)

        a = split(x_ref[k0 + SB : NB, 0:NB])
        x_ref[k0 + SB : NB, :] = x_ref[k0 + SB : NB, :] - dot3(a, (pad(zh), pad(zl)))


def tiled(x):
    return jnp.concatenate([x] * (N // NB), 1)


def factor_all(g_refs, x_refs, p_refs, s_refs, w_refs, l_refs, e_refs, scale_refs):
    r_i = lax.broadcasted_iota(jnp.int32, (NB, NB), 0)
    c_i = lax.broadcasted_iota(jnp.int32, (NB, NB), 1)
    wide = lax.broadcasted_iota(jnp.int32, (NB, N), 1)
    for l_ref in l_refs:
        l_ref[...] = jnp.zeros_like(l_ref)

    def outer(o, carry):
        base = pl.multiple_of(o * NB, NB)
        here = pl.ds(base, NB)
        for g_ref, x_ref in zip(g_refs, x_refs):
            x_ref[:, 0:NB] = g_ref[here, here]
            x_ref[:, NB : 2 * NB] = jnp.where(r_i == c_i, 1.0, 0.0)
        for s in range(NB // SB):
            for x_ref, p_ref, s_ref in zip(x_refs, p_refs, s_refs):
                eliminate(s, x_ref, p_ref, s_ref)
        for m in range(2):
            p_ref, s_ref, w_ref = p_refs[m], s_refs[m], w_refs[m]
            l_refs[m][here, here] = jnp.where(r_i >= c_i, p_ref[:, 0:NB].T, 0.0)
            inverse = p_ref[:, NB : 2 * NB]
            w_ref[...] = dot3(split(inverse), split(g_refs[m][here, :]))
            w_ref[:, here] = inverse
            unit = w_ref[...] * tiled(s_ref[:, NB : 2 * NB])
            e_refs[m][here, :] = jnp.where(wide < base + NB, unit, 0.0).astype(BF16)
            scale_refs[m][here, :] = s_ref[:, 0:NB]
        for p in range(1, N // NB):
            rows = slice(p * NB, (p + 1) * NB)

            @pl.when(p > o)
            def _():
                for g_ref, p_ref, w_ref, l_ref in zip(g_refs, p_refs, w_refs, l_refs):
                    lower = dot3(split(g_ref[rows, here]), split(p_ref[:, NB : 2 * NB]), 1)
                    l_ref[rows, here] = lower
                    g_ref[rows, here] = jnp.zeros((NB, NB), F32)
                    g_ref[rows, :] = g_ref[rows, :] - dot3(split(lower), split(w_ref[...]))

        return carry

    lax.fori_loop(0, N // NB, outer, 0)


LOWER = [(r, c) for r in range(N // NB) for c in range(r)]
TAIL = 8 * NB
PACKED = TAIL + SB


def block(ref, r, c):
    return ref[r * NB : (r + 1) * NB, c * NB : (c + 1) * NB]


def at(first, b):
    return slice(first + b * NB, first + (b + 1) * NB)


def iotas():
    return (
        lax.broadcasted_iota(jnp.int32, (NB, NB), 0),
        lax.broadcasted_iota(jnp.int32, (NB, NB), 1),
    )


def pick_rows(rows):
    where = lax.broadcasted_iota(jnp.int32, (SB, NB), 0)
    tile = jnp.zeros((SB, NB), F32)
    for k, row in enumerate(rows):
        tile = jnp.where(where == k, jnp.broadcast_to(row, (SB, NB)), tile)
    return tile


def pack_unit(e_ref, scale_ref, dst_ref):
    r_i, c_i = iotas()
    for b, (r, c) in enumerate(LOWER):
        dst_ref[at(0, b), :] = block(e_ref, r, c)
    for k in range(2):
        one = block(e_ref, 2 * k, 2 * k).astype(F32)
        two = block(e_ref, 2 * k + 1, 2 * k + 1).astype(F32).T
        dst_ref[at(0, 6 + k), :] = jnp.where(r_i > c_i, one, jnp.where(r_i < c_i, two, 0.0)).astype(BF16)
    parts = [[], [], []]
    for k in range(N // NB):
        rest = scale_ref[k * NB : (k + 1) * NB, :].T[0:1, :]
        for part in parts:
            part.append(rest)
            rest = rest - rest.astype(BF16).astype(F32)
    dst_ref[TAIL:PACKED, :] = pick_rows(sum(parts, [])).astype(BF16)


def unpack_unit(src_ref, e_ref, scale_ref, row_ref):
    r_i, c_i = iotas()
    eye = jnp.where(r_i == c_i, 1.0, 0.0)
    zero = jnp.zeros((NB, NB), BF16)
    for b, (r, c) in enumerate(LOWER):
        e_ref[r * NB : (r + 1) * NB, c * NB : (c + 1) * NB] = src_ref[at(0, b), :]
        e_ref[c * NB : (c + 1) * NB, r * NB : (r + 1) * NB] = zero
    for k in range(2):
        pair = src_ref[at(0, 6 + k), :].astype(F32)
        for d, value in ((2 * k, pair), (2 * k + 1, pair.T)):
            e_ref[d * NB : (d + 1) * NB, d * NB : (d + 1) * NB] = jnp.where(r_i > c_i, value, eye).astype(BF16)
    tile = src_ref[TAIL:PACKED, :].astype(F32)
    for k in range(N // NB):
        row = tile[k : k + 1, :] + tile[4 + k : 5 + k, :] + tile[8 + k : 9 + k, :]
        row_ref[:, k * NB : (k + 1) * NB] = jnp.broadcast_to(row, (8, NB))
        scale_ref[k * NB : (k + 1) * NB, :] = jnp.broadcast_to(row, (NB, NB)).T


def scale_row(scale_ref, row_ref):
    for k in range(N // NB):
        row_ref[:, k * NB : (k + 1) * NB] = scale_ref[k * NB : (k + 1) * NB, :].T[0:8, :]


def pack_symmetric(value, dst_ref):
    r_i, c_i = iotas()
    for b, (r, c) in enumerate(LOWER):
        dst_ref[at(0, b), :] = block(value, r, c).astype(BF16)
    rows = []
    for k in range(2):
        two = block(value, 2 * k + 1, 2 * k + 1)
        dst_ref[at(0, 6 + k), :] = jnp.where(r_i >= c_i, block(value, 2 * k, 2 * k), two).astype(BF16)
        rows.append(jnp.sum(jnp.where(r_i == c_i, two, 0.0), 0, keepdims=True))
    dst_ref[TAIL:PACKED, :] = pick_rows(rows).astype(BF16)


def add_symmetric(src_ref, dst_ref):
    r_i, c_i = iotas()

    def sub(r, c, value):
        rows, cols = slice(r * NB, (r + 1) * NB), slice(c * NB, (c + 1) * NB)
        dst_ref[rows, cols] = dst_ref[rows, cols] - value

    for b, (r, c) in enumerate(LOWER):
        value = src_ref[at(0, b), :].astype(F32)
        sub(r, c, value)
        sub(c, r, value.T)
    tile = src_ref[TAIL:PACKED, :].astype(F32)
    for k in range(2):
        pair = src_ref[at(0, 6 + k), :].astype(F32)
        turned = pair.T
        sub(2 * k, 2 * k, jnp.where(r_i >= c_i, pair, turned))
        diagonal = jnp.broadcast_to(tile[k : k + 1, :], (NB, NB))
        two = jnp.where(r_i < c_i, pair, turned)
        sub(2 * k + 1, 2 * k + 1, jnp.where(r_i == c_i, diagonal, two))


def solve_t(e_ref, row_ref, c_ref, out_ref):
    h = N // 2
    row = row_ref[0:1, :]
    out_ref[:, 0:h] = (dot(c_ref[:, 0:h], e_ref[0:h, 0:h], 1, 1) * row[:, 0:h]).astype(BF16)
    out_ref[:, h:N] = (dot(c_ref[...], e_ref[h:N, :], 1, 1) * row[:, h:N]).astype(BF16)


def solve_n(e_ref, scale_ref, c_ref, out_ref):
    h = N // 2
    out_ref[0:h, :] = (dot(e_ref[0:h, 0:h], c_ref[0:h, :]) * tiled(scale_ref[0:h, :])).astype(BF16)
    out_ref[h:N, :] = (dot(e_ref[h:N, :], c_ref[...]) * tiled(scale_ref[h:N, :])).astype(BF16)


ANY = pl.BlockSpec(memory_space=pl.ANY)
VM = pl.BlockSpec(memory_space=pltpu.VMEM)
B16 = pltpu.VMEM((N, N), BF16)
WIDE = pltpu.VMEM((N, N), F32)


def shape(dims, kind):
    return jax.ShapeDtypeStruct(dims, kind)


def call(kernel, outs, in_specs, out_specs, scratch, flops, limit, aliases=None):
    return pl.pallas_call(
        kernel,
        out_shape=outs,
        in_specs=in_specs,
        out_specs=out_specs,
        scratch_shapes=scratch,
        input_output_aliases=aliases or {},
        compiler_params=pltpu.CompilerParams(vmem_limit_bytes=limit << 20),
        cost_estimate=pl.CostEstimate(flops=flops * 10**9, bytes_accessed=4 << 20, transcendentals=0),
    )


def factor_kernel(d_ref, l_out, e0, e1, scale0, scale1, packed,
                  g0, g1, x0, x1, p0, p1, s0, s1, w0, w1, l0, l1, in_sem, out_sem):
    copies = [
        pltpu.make_async_copy(d_ref.at[0, 0], g0, in_sem.at[0]),
        pltpu.make_async_copy(d_ref.at[1, 1], g1, in_sem.at[1]),
    ]
    for c in copies:
        c.start()
    for c in copies:
        c.wait()
    factor_all((g0, g1), (x0, x1), (p0, p1), (s0, s1), (w0, w1), (l0, l1), (e0, e1), (scale0, scale1))
    outs = [
        pltpu.make_async_copy(l0, l_out.at[0, 0], out_sem.at[0]),
        pltpu.make_async_copy(l1, l_out.at[1, 0], out_sem.at[1]),
    ]
    for c in outs:
        c.start()
    pack_unit(e0, scale0, packed)
    for c in outs:
        c.wait()


def factor_call(diag_blocks):
    half = pltpu.VMEM((NB, 2 * NB), F32)
    return call(
        factor_kernel,
        (shape((2, 1, N, N), F32), shape((N, N), BF16), shape((N, N), BF16),
         shape((N, NB), F32), shape((N, NB), F32), shape((PACKED, NB), BF16)),
        [ANY], (ANY, VM, VM, VM, VM, VM),
        [WIDE, WIDE] + [half] * 6 + [pltpu.VMEM((NB, N), F32)] * 2 + [WIDE, WIDE]
        + [pltpu.SemaphoreType.DMA((2,)), pltpu.SemaphoreType.DMA((2,))],
        60, 20,
    )(diag_blocks)


def local_kernel(d_ref, h_ref, v_ref, e0, e1, scale0, scale1, to_right, to_below, sbuf, dbuf, link_out,
                 hh, hv, y0, y1, y2, y3, z2, z3, lbuf, row1, in_sem, out_sem):
    copies = [
        pltpu.make_async_copy(h_ref, hh, in_sem.at[0]),
        pltpu.make_async_copy(v_ref, hv, in_sem.at[1]),
        pltpu.make_async_copy(d_ref.at[0, 1], sbuf.at[0], in_sem.at[2]),
        pltpu.make_async_copy(d_ref.at[1, 0], sbuf.at[1], in_sem.at[3]),
    ]
    for c in copies:
        c.start()
    for c in copies[:2]:
        c.wait()
    scale_row(scale1, row1)
    solve_n(e1, scale1, hh.at[1, 1], y2)
    solve_n(e1, scale1, hv.at[1, 1], y3)
    t2 = y2[...].T
    pack_symmetric(dot(t2, y2[...]), to_right)
    side = dot(t2, y3[...])
    for r in range(N // NB):
        for c in range(N // NB):
            to_right[at(PACKED, 4 * r + c), :] = block(side, r, c).astype(BF16)
    pack_symmetric(dot(y3[...].T, y3[...]), to_below)
    solve_t(e1, row1, hh.at[1, 0], y0)
    solve_t(e1, row1, hv.at[0, 1], y1)
    solve_n(e0, scale0, hh.at[0, 0], z2)
    solve_n(e0, scale0, hv.at[0, 0], z3)
    u2 = z2[...].T
    for c in copies[2:]:
        c.wait()
    outs = []

    def link(slot, row, which, value):
        lbuf[slot] = (-value).astype(BF16)
        copy = pltpu.make_async_copy(lbuf.at[slot], link_out.at[row, 0, which], out_sem.at[slot])
        copy.start()
        outs.append(copy)

    link(0, 0, 1, dot(y1[...], y3[...]))
    link(1, 0, 3, dot(u2, z3[...]) + dot(y1[...], y0[...], 1, 1))
    link(2, 1, 0, dot(y0[...], y2[...]))
    dbuf[0] = dot(y1[...], y2[...])
    dbuf[1] = dot(y0[...], y3[...])
    sbuf[0] = sbuf[0] - (dot(u2, z2[...]) + dot(y1[...], y1[...], 1, 1))
    sbuf[1] = sbuf[1] - (dot(z3[...].T, z3[...]) + dot(y0[...], y0[...], 1, 1))
    for c in outs:
        c.wait()


def local_call(*args):
    return call(
        local_kernel,
        (shape((PACKED + N * N // NB, NB), BF16), shape((PACKED, NB), BF16), shape((2, N, N), F32),
         shape((2, N, N), F32), shape((2, 1, 4, N, N), BF16)),
        [ANY] * 3 + [VM] * 4, (VM, VM, VM, VM, ANY),
        [pltpu.VMEM((2, 2, N, N), BF16)] * 2 + [B16] * 6
        + [pltpu.VMEM((3, N, N), BF16), pltpu.VMEM((8, N), F32)]
        + [pltpu.SemaphoreType.DMA((4,)), pltpu.SemaphoreType.DMA((3,))],
        12, 28,
    )(*args)


def across_kernel(h_ref, v_ref, rpack, bpack, rc, bc, bc0, se, schur_in, link_in, schur_out, sw, link_out,
                  inv_a, inv_b, c0, c1, ra0, r2, r3, b0, b1, b2, b3, scale_a, scale_b, row_a, row_b,
                  lbuf, in_sem, sem):
    loads = [
        pltpu.make_async_copy(h_ref.at[0, 1], c0, in_sem.at[0]),
        pltpu.make_async_copy(v_ref.at[1, 0], c1, in_sem.at[1]),
    ]
    for c in loads:
        c.start()
    unpack_unit(rpack, inv_a, scale_a, row_a)
    unpack_unit(bpack, inv_b, scale_b, row_b)
    for c in loads:
        c.wait()
    outs = []

    def link(slot, row, which, value):
        lbuf[slot] = (-value).astype(BF16)
        copy = pltpu.make_async_copy(lbuf.at[slot], link_out.at[row, 0, which], sem.at[slot])
        copy.start()
        outs.append(copy)

    solve_t(inv_a, row_a, c0, ra0)
    solve_n(inv_a, scale_a, rc.at[0], r2)
    solve_n(inv_a, scale_a, rc.at[1], r3)
    link(0, 0, 0, dot(ra0[...], r2[...]))
    link(1, 0, 2, dot(ra0[...], r3[...]) + se[0])
    solve_t(inv_b, row_b, c1, b1)
    solve_n(inv_b, scale_b, bc.at[1], b3)
    link(2, 1, 1, dot(b1[...], b3[...]))
    solve_n(inv_b, scale_b, bc.at[0], b2)
    link(3, 1, 2, dot(b1[...], b2[...]) + se[1])
    solve_t(inv_b, row_b, bc0, b0)
    schur_out[0] = schur_in[0] - dot(ra0[...], ra0[...], 1, 1)
    schur_out[1] = schur_in[1] - dot(b1[...], b1[...], 1, 1)
    sw[...] = dot(b1[...], b0[...], 1, 1)
    for c in outs:
        c.wait()


def across_call(*args):
    return call(
        across_kernel,
        (shape((2, N, N), F32), shape((N, N), F32), shape((2, 1, 4, N, N), BF16)),
        [ANY] * 2 + [VM] * 7 + [ANY], (VM, VM, ANY),
        [B16] * 11 + [pltpu.VMEM((N, NB), F32)] * 2 + [pltpu.VMEM((8, N), F32)] * 2
        + [pltpu.VMEM((4, N, N), BF16), pltpu.SemaphoreType.DMA((2,)), pltpu.SemaphoreType.DMA((4,))],
        10, 30, {9: 2},
    )(*args)


def last_kernel(from_left, from_above, schur_in, sw, link_in, schur_out, link_out, sbuf, lbuf, sem):
    lbuf[...] = jnp.concatenate(
        [
            jnp.concatenate(
                [
                    (-(block(sw, r, c) + from_left[at(PACKED, 4 * r + c), :].astype(F32))).astype(BF16)
                    for c in range(N // NB)
                ],
                1,
            )
            for r in range(N // NB)
        ],
        0,
    )
    outs = [
        pltpu.make_async_copy(lbuf, link_out.at[1, 0, 3], sem.at[0]),
        pltpu.make_async_copy(sbuf.at[0], schur_out.at[0, 0], sem.at[1]),
        pltpu.make_async_copy(sbuf.at[1], schur_out.at[1, 0], sem.at[2]),
    ]
    outs[0].start()
    for m, src in enumerate((from_above, from_left)):
        sbuf[m] = schur_in[m]
        add_symmetric(src, sbuf.at[m])
        outs[1 + m].start()
    for c in outs:
        c.wait()


def last_call(*args):
    return call(
        last_kernel,
        (shape((2, 1, N, N), F32), shape((2, 1, 4, N, N), BF16)),
        [VM] * 4 + [ANY], (ANY, ANY),
        [pltpu.VMEM((2, N, N), F32), B16, pltpu.SemaphoreType.DMA((3,))],
        2, 16, {4: 1},
    )(*args)


def passed(value, down, right):
    rows, cols = lax.axis_size("row"), lax.axis_size("col")
    if not right:
        return lax.ppermute(value, "row", [(i, (i + down) % rows) for i in range(rows)])
    if not down:
        return lax.ppermute(value, "col", [(i, (i + right) % cols) for i in range(cols)])
    pairs = [(r * cols + c, ((r + down) % rows) * cols + (c + right) % cols) for r in range(rows) for c in range(cols)]
    return lax.ppermute(value, ("row", "col"), pairs)


def on_device(diag_blocks, horizontal, vertical):
    pair = jnp.stack([horizontal[0, 0], vertical[0, 0]])
    below = passed(pair, -1, 0)
    right = passed(pair, 0, -1)
    below0 = passed(horizontal[0, 1], -1, 1)
    factor, e0, e1, scale0, scale1, packed = factor_call(diag_blocks)
    below_inverse = passed(packed, -1, 0)
    right_inverse = passed(packed, 0, -1)
    to_right, to_below, schur, southeast, links = local_call(diag_blocks, horizontal, vertical, e0, e1, scale0, scale1)
    from_left = passed(to_right, 0, 1)
    from_above = passed(to_below, 1, 0)
    schur, southwest, links = across_call(
        horizontal, vertical, right_inverse, below_inverse, right, below, below0,
        southeast, schur, links,
    )
    schur, links = last_call(from_left, from_above, schur, southwest, links)
    return (factor, schur, links)


def solution(mesh):
    blocks = P("row", "col", None, None)
    return jax.shard_map(
        on_device,
        mesh=mesh,
        in_specs=(blocks, blocks, blocks),
        out_specs=(blocks, blocks, P("row", "col", None, None, None)),
        check_vma=False,
    )
```

profile of v0, /device:TPU:0, one launch (start us, length us, event | category | flops | bytes accessed | tf_op | source)
XLA Modules:
  0.0 77.5 jit_solution(1775674621792996089)
XLA Ops:
  0.6 1.1 %slice_bitcast_fusion.1 = bf16[1,512,512]{2,1,0:T(8,128)(2,1)S(1)} fusion(bf16[2,2,512,512]{3,2,1,0:T(8,128)(2,1)} %v_ref.3), kind=kLoop, calls=%fused_computation.2 | loop fusion | bytes 1048576 | tf_op jit(solution)/shard_map/stack;squeeze | solution.py:462
  1.7 0.0 copy-start.2
  1.7 1.4 %slice_bitcast_fusion = (bf16[512,512]{1,0:T(8,128)(2,1)S(1)}, bf16[1,512,512]{2,1,0:T(8,128)(2,1)S(1)}) fusion(bf16[2,2,512,512]{3,2,1,0:T(8,128)(2,1)} %h_ref.3), kind=kLoop, calls=%fused_computation.1 | loop fusion | bytes 2097152 | tf_op jit(solution)/shard_map/squeeze | solution.py:465
  3.1 0.1 pad_maximum_fusion
  3.3 0.0 copy-start
  3.3 0.0 copy-start.1
  3.3 6.7 %collective-permute-start.5 = (bf16[2,512,512]{2,1,0:T(8,128)(2,1)S(1)}, bf16[2,512,512]{2,1,0:T(8,128)(2,1)S(1)}, u32[]{:S(2)}, u32[]{:S(2)}) collective-permute-start(bf16[2,512,512]{2,1,0:T(8,128)(2,1)S(1)} %pad_maximum_fusion), channel_id=1, source_target_pairs={{0,112},{16,0},{32,16},{48,32},{64,48},{80,64},{96,80},{112,96},{1... | collective-permute-start | bytes 3145736 | tf_op jit(solution)/shard_map/ppermute | solution.py:454
  10.0 2.2 %collective-permute-start.4 = (bf16[2,512,512]{2,1,0:T(8,128)(2,1)S(1)}, bf16[2,512,512]{2,1,0:T(8,128)(2,1)S(1)}, u32[]{:S(2)}, u32[]{:S(2)}) collective-permute-start(bf16[2,512,512]{2,1,0:T(8,128)(2,1)S(1)} %pad_maximum_fusion), channel_id=1, source_target_pairs={{0,15},{1,0},{2,1},{3,2},{4,3},{5,4},{6,5},{7,6},{8,7},{9,8},{10,9... | collective-permute-start | bytes 3145736 | tf_op jit(solution)/shard_map/ppermute | solution.py:456
  12.2 23.7 %shard_map.58 = (f32[2,1,512,512]{3,2,1,0:T(8,128)}, bf16[512,512]{1,0:T(8,128)(2,1)S(1)}, bf16[512,512]{1,0:T(8,128)(2,1)S(1)}, f32[512,128]{1,0:T(8,128)S(1)},...) custom-call(f32[2,2,512,512]{3,2,1,0:T(8,128)S(1)} %copy-done.2), custom_call_target="tpu_custom_call" | custom-call | flops 60000002048 | bytes 4194304 | tf_op jit(solution)/shard_map/pallas_call | solution.py:291
  35.9 2.1 %collective-permute-start.3 = (bf16[1040,128]{1,0:T(8,128)(2,1)S(1)}, bf16[1040,128]{1,0:T(8,128)(2,1)S(1)}, u32[]{:S(2)}, u32[]{:S(2)}) collective-permute-start(bf16[1040,128]{1,0:T(8,128)(2,1)S(1)} %get-tuple-element.26), channel_id=1, source_target_pairs={{0,112},{16,0},{32,16},{48,32},{64,48},{80,64},{96,80},{112,96},{1... | collective-permute-start | bytes 798728 | tf_op jit(solution)/shard_map/ppermute | solution.py:454
  38.0 0.1 collective-permute-start.2
  38.0 1.4 %collective-permute-start.6 = (bf16[512,512]{1,0:T(8,128)(2,1)S(1)}, bf16[512,512]{1,0:T(8,128)(2,1)S(1)}, u32[]{:S(2)}, u32[]{:S(2)}) collective-permute-start(bf16[512,512]{1,0:T(8,128)(2,1)S(1)} %get-tuple-element.35), channel_id=1, source_target_pairs={{0,113},{1,114},{2,115},{3,116},{4,117},{5,118},{6,119},{7,120},{8... | collective-permute-start | bytes 1572872 | tf_op jit(solution)/shard_map/ppermute | solution.py:458
  39.5 5.6 %shard_map.59 = (bf16[3088,128]{1,0:T(8,128)(2,1)S(1)}, bf16[1040,128]{1,0:T(8,128)(2,1)S(1)}, f32[2,512,512]{2,1,0:T(8,128)S(1)}, f32[2,512,512]{2,1,0:T(8,128)S(1)}, bf16[2,1,4,512,512]{4,3,2,1,0:T(8,128)(2,1)}) custom-call(f32[2,2,512,512]{3,2,1,0:T(8,128)S(1)} %copy-done.2, bf16[2,2,512,512]{3,2,1,0:T(8,128)(2,1)S(1)} %copy-done, ...), custom_call_target="tpu_custom_call" | custom-call | flops 12000000000 | bytes 4194304 | tf_op jit(solution)/shard_map/pallas_call | solution.py:351
  45.1 7.1 %collective-permute-done.3.bpack = bf16[1040,128]{1,0:T(8,128)(2,1)S(1)} collective-permute-done((bf16[1040,128]{1,0:T(8,128)(2,1)S(1)}, bf16[1040,128]{1,0:T(8,128)(2,1)S(1)}, u32[]{:S(2)}, u32[]{:S(2)}) %collective-permute-start.3) | collective-permute-done | bytes 266272 | tf_op jit(solution)/shard_map/ppermute | solution.py:454
  52.2 1.2 %collective-permute-start.1 = (bf16[1040,128]{1,0:T(8,128)(2,1)S(1)}, bf16[1040,128]{1,0:T(8,128)(2,1)S(1)}, u32[]{:S(2)}, u32[]{:S(2)}) collective-permute-start(bf16[1040,128]{1,0:T(8,128)(2,1)S(1)} %get-tuple-element.25), channel_id=1, source_target_pairs={{0,16},{16,32},{32,48},{48,64},{64,80},{80,96},{96,112},{112,0},{1... | collective-permute-start | bytes 798728 | tf_op jit(solution)/shard_map/ppermute | solution.py:454
  53.3 1.7 %collective-permute-done.2.rpack = bf16[1040,128]{1,0:T(8,128)(2,1)S(1)} collective-permute-done((bf16[1040,128]{1,0:T(8,128)(2,1)S(1)}, bf16[1040,128]{1,0:T(8,128)(2,1)S(1)}, u32[]{:S(2)}, u32[]{:S(2)}) %collective-permute-start.2) | collective-permute-done | bytes 266272 | tf_op jit(solution)/shard_map/ppermute | solution.py:456
  55.0 1.2 %collective-permute-start = (bf16[3088,128]{1,0:T(8,128)(2,1)S(1)}, bf16[3088,128]{1,0:T(8,128)(2,1)S(1)}, u32[]{:S(2)}, u32[]{:S(2)}) collective-permute-start(bf16[3088,128]{1,0:T(8,128)(2,1)S(1)} %get-tuple-element.24), channel_id=1, source_target_pairs={{0,1},{1,2},{2,3},{3,4},{4,5},{5,6},{6,7},{7,8},{8,9},{9,10},{10,1... | collective-permute-start | bytes 2371592 | tf_op jit(solution)/shard_map/ppermute | solution.py:456
  56.2 8.5 %collective-permute-done.6.bc0 = bf16[512,512]{1,0:T(8,128)(2,1)S(1)} collective-permute-done((bf16[512,512]{1,0:T(8,128)(2,1)S(1)}, bf16[512,512]{1,0:T(8,128)(2,1)S(1)}, u32[]{:S(2)}, u32[]{:S(2)}) %collective-permute-start.6) | collective-permute-done | bytes 524320 | tf_op jit(solution)/shard_map/ppermute | solution.py:458
  64.7 0.0 collective-permute-done.5.bc
  64.7 0.0 collective-permute-done.4.rc
  64.7 4.2 %shard_map.60 = (f32[2,512,512]{2,1,0:T(8,128)S(1)}, f32[512,512]{1,0:T(8,128)S(1)}, bf16[2,1,4,512,512]{4,3,2,1,0:T(8,128)(2,1)}) custom-call(bf16[2,2,512,512]{3,2,1,0:T(8,128)(2,1)S(1)} %copy-done, bf16[2,2,512,512]{3,2,1,0:T(8,128)(2,1)S(1)} %copy-done.1, bf16[1040,128]{1,0:T(8,128)(2,1)S(1)} %collective-permute-done.2.rpack, ...), custom_call_target="tpu_custom_call", output_to_operand_aliasing={{2}: (9, {})} | custom-call | flops 10000000000 | bytes 4194304 | tf_op jit(solution)/shard_map/pallas_call | solution.py:403
  68.9 1.5 %collective-permute-done.1.from_above = bf16[1040,128]{1,0:T(8,128)(2,1)S(1)} collective-permute-done((bf16[1040,128]{1,0:T(8,128)(2,1)S(1)}, bf16[1040,128]{1,0:T(8,128)(2,1)S(1)}, u32[]{:S(2)}, u32[]{:S(2)}) %collective-permute-start.1) | collective-permute-done | bytes 266272 | tf_op jit(solution)/shard_map/ppermute | solution.py:454
  70.4 5.1 %collective-permute-done.from_left = bf16[3088,128]{1,0:T(8,128)(2,1)S(1)} collective-permute-done((bf16[3088,128]{1,0:T(8,128)(2,1)S(1)}, bf16[3088,128]{1,0:T(8,128)(2,1)S(1)}, u32[]{:S(2)}, u32[]{:S(2)}) %collective-permute-start) | collective-permute-done | bytes 790560 | tf_op jit(solution)/shard_map/ppermute | solution.py:456
  75.5 1.8 %shard_map.61 = (f32[2,1,512,512]{3,2,1,0:T(8,128)}, bf16[2,1,4,512,512]{4,3,2,1,0:T(8,128)(2,1)}) custom-call(bf16[3088,128]{1,0:T(8,128)(2,1)S(1)} %collective-permute-done.from_left, bf16[1040,128]{1,0:T(8,128)(2,1)S(1)} %collective-permute-done.1.from_above, f32[2,512,512]{2,1,0:T(8,128)S(1)} %get-tuple-element.30.schur_in, ...), custom_call_target="tpu_custom_call", output_to_operand_aliasing={{1}: (4, {})} | custom-call | flops 2000000000 | bytes 4194304 | tf_op jit(solution)/shard_map/pallas_call | solution.py:442
  (3 shorter events, 0.0 us)
Async XLA Ops:
  1.7 10.5 %copy-start.2 = (f32[2,2,512,512]{3,2,1,0:T(8,128)S(1)}, f32[2,2,512,512]{3,2,1,0:T(8,128)}, u32[]{:S(2)}) copy-start(f32[2,2,512,512]{3,2,1,0:T(8,128)} %d_ref.3) | copy-start | bytes 12582916
  3.3 36.2 %copy-start = (bf16[2,2,512,512]{3,2,1,0:T(8,128)(2,1)S(1)}, bf16[2,2,512,512]{3,2,1,0:T(8,128)(2,1)}, u32[]{:S(2)}) copy-start(bf16[2,2,512,512]{3,2,1,0:T(8,128)(2,1)} %h_ref.3) | copy-start | bytes 6291460
  3.3 36.2 %copy-start.1 = (bf16[2,2,512,512]{3,2,1,0:T(8,128)(2,1)S(1)}, bf16[2,2,512,512]{3,2,1,0:T(8,128)(2,1)}, u32[]{:S(2)}) copy-start(bf16[2,2,512,512]{3,2,1,0:T(8,128)(2,1)} %v_ref.3) | copy-start | bytes 6291460
  3.3 61.4 %collective-permute-start.5 = (bf16[2,512,512]{2,1,0:T(8,128)(2,1)S(1)}, bf16[2,512,512]{2,1,0:T(8,128)(2,1)S(1)}, u32[]{:S(2)}, u32[]{:S(2)}) collective-permute-start(bf16[2,512,512]{2,1,0:T(8,128)(2,1)S(1)} %pad_maximum_fusion), channel_id=1, source_target_pairs={{0,112},{16,0},{32,16},{48,32},{64,48},{80,64},{96,80},{112,96},{1... | collective-permute-start | bytes 3145736 | tf_op jit(solution)/shard_map/ppermute | solution.py:454
  10.0 54.7 %collective-permute-start.4 = (bf16[2,512,512]{2,1,0:T(8,128)(2,1)S(1)}, bf16[2,512,512]{2,1,0:T(8,128)(2,1)S(1)}, u32[]{:S(2)}, u32[]{:S(2)}) collective-permute-start(bf16[2,512,512]{2,1,0:T(8,128)(2,1)S(1)} %pad_maximum_fusion), channel_id=1, source_target_pairs={{0,15},{1,0},{2,1},{3,2},{4,3},{5,4},{6,5},{7,6},{8,7},{9,8},{10,9... | collective-permute-start | bytes 3145736 | tf_op jit(solution)/shard_map/ppermute | solution.py:456
  35.9 16.3 %collective-permute-start.3 = (bf16[1040,128]{1,0:T(8,128)(2,1)S(1)}, bf16[1040,128]{1,0:T(8,128)(2,1)S(1)}, u32[]{:S(2)}, u32[]{:S(2)}) collective-permute-start(bf16[1040,128]{1,0:T(8,128)(2,1)S(1)} %get-tuple-element.26), channel_id=1, source_target_pairs={{0,112},{16,0},{32,16},{48,32},{64,48},{80,64},{96,80},{112,96},{1... | collective-permute-start | bytes 798728 | tf_op jit(solution)/shard_map/ppermute | solution.py:454
  38.0 17.0 %collective-permute-start.2 = (bf16[1040,128]{1,0:T(8,128)(2,1)S(1)}, bf16[1040,128]{1,0:T(8,128)(2,1)S(1)}, u32[]{:S(2)}, u32[]{:S(2)}) collective-permute-start(bf16[1040,128]{1,0:T(8,128)(2,1)S(1)} %get-tuple-element.26), channel_id=1, source_target_pairs={{0,15},{1,0},{2,1},{3,2},{4,3},{5,4},{6,5},{7,6},{8,7},{9,8},{10,9... | collective-permute-start | bytes 798728 | tf_op jit(solution)/shard_map/ppermute | solution.py:456
  38.0 26.6 %collective-permute-start.6 = (bf16[512,512]{1,0:T(8,128)(2,1)S(1)}, bf16[512,512]{1,0:T(8,128)(2,1)S(1)}, u32[]{:S(2)}, u32[]{:S(2)}) collective-permute-start(bf16[512,512]{1,0:T(8,128)(2,1)S(1)} %get-tuple-element.35), channel_id=1, source_target_pairs={{0,113},{1,114},{2,115},{3,116},{4,117},{5,118},{6,119},{7,120},{8... | collective-permute-start | bytes 1572872 | tf_op jit(solution)/shard_map/ppermute | solution.py:458
  52.2 18.2 %collective-permute-start.1 = (bf16[1040,128]{1,0:T(8,128)(2,1)S(1)}, bf16[1040,128]{1,0:T(8,128)(2,1)S(1)}, u32[]{:S(2)}, u32[]{:S(2)}) collective-permute-start(bf16[1040,128]{1,0:T(8,128)(2,1)S(1)} %get-tuple-element.25), channel_id=1, source_target_pairs={{0,16},{16,32},{32,48},{48,64},{64,80},{80,96},{96,112},{112,0},{1... | collective-permute-start | bytes 798728 | tf_op jit(solution)/shard_map/ppermute | solution.py:454
  55.0 20.4 %collective-permute-start = (bf16[3088,128]{1,0:T(8,128)(2,1)S(1)}, bf16[3088,128]{1,0:T(8,128)(2,1)S(1)}, u32[]{:S(2)}, u32[]{:S(2)}) collective-permute-start(bf16[3088,128]{1,0:T(8,128)(2,1)S(1)} %get-tuple-element.24), channel_id=1, source_target_pairs={{0,1},{1,2},{2,3},{3,4},{4,5},{5,6},{6,7},{7,8},{8,9},{9,10},{10,1... | collective-permute-start | bytes 2371592 | tf_op jit(solution)/shard_map/ppermute | solution.py:456
where the time goes:
time: 77.6 us; the launch traced here: 77.5 us
  Pallas kernels  35.4 us (46%)
  waiting for transfers between devices  23.9 us (31%)
  starting transfers between devices  14.8 us (19%)
  local copies, waits for them, and re-layouts  2.52 us (3%)
  between operations  0.86 us (1%)
    pallas_call x1, Pallas kernels, factor_call(): call(factor_kernel, (shape((2, 1, N, N), F32), shape((N, N), BF16), shape...  23.7 us
    ppermute x3, starting transfers between devices, passed(): lax.ppermute(value, 'row', [(i, (i + down) % rows) for i in range(rows)])  9.93 us
    ppermute x3, waiting for transfers between devices, passed(): lax.ppermute(value, 'row', [(i, (i + down) % rows) for i in range(rows)])  8.6 us
    ppermute x1, waiting for transfers between devices, passed(): return lax.ppermute(value, ('row', 'col'), pairs)  8.51 us
    ppermute x3, waiting for transfers between devices, passed(): lax.ppermute(value, 'col', [(i, (i + right) % cols) for i in range(cols)])  6.75 us
    pallas_call x1, Pallas kernels, local_call(): call(local_kernel, (shape((PACKED + N * N // NB, NB), BF16), shape((PACKE...  5.64 us
    pallas_call x1, Pallas kernels, across_call(): call(across_kernel, (shape((2, N, N), F32), shape((N, N), F32), shape((2,...  4.16 us
    ppermute x3, starting transfers between devices, passed(): lax.ppermute(value, 'col', [(i, (i + right) % cols) for i in range(cols)])  3.44 us
  transfers between devices with their start and end apart: 7, of which 5 were waited for; matrix products, arithmetic and copies ran while one was open for 0% of the time, Pallas kernels for 43%

commit v1 on v0

--- a/solution.py
+++ b/solution.py
@@ -86,7 +86,7 @@
     return jnp.concatenate([x] * (N // NB), 1)
 
 
-def factor_all(g_refs, x_refs, p_refs, s_refs, w_refs, l_refs, e_refs, scale_refs):
+def factor_steps(first, last, g_refs, x_refs, p_refs, s_refs, w_refs, l_refs, e_refs, scale_refs):
     r_i = lax.broadcasted_iota(jnp.int32, (NB, NB), 0)
     c_i = lax.broadcasted_iota(jnp.int32, (NB, NB), 1)
     wide = lax.broadcasted_iota(jnp.int32, (NB, N), 1)
@@ -111,7 +111,7 @@
             unit = w_ref[...] * tiled(s_ref[:, NB : 2 * NB])
             e_refs[m][here, :] = jnp.where(wide < base + NB, unit, 0.0).astype(BF16)
             scale_refs[m][here, :] = s_ref[:, 0:NB]
-        for p in range(1, N // NB):
+        for p in range(first + 1, N // NB):
             rows = slice(p * NB, (p + 1) * NB)
 
             @pl.when(p > o)
@@ -124,7 +124,7 @@
 
         return carry
 
-    lax.fori_loop(0, N // NB, outer, 0)
+    lax.fori_loop(first, last, outer, 0)
 
 
 LOWER = [(r, c) for r in range(N // NB) for c in range(r)]
@@ -264,8 +264,13 @@
     )
 
 
-def factor_kernel(d_ref, l_out, e0, e1, scale0, scale1, packed,
-                  g0, g1, x0, x1, p0, p1, s0, s1, w0, w1, l0, l1, in_sem, out_sem):
+H = N // 2
+HALF = [pltpu.VMEM((NB, 2 * NB), F32)] * 6 + [pltpu.VMEM((NB, N), F32)] * 2
+DMA2 = pltpu.SemaphoreType.DMA((2,))
+
+
+def first_kernel(d_ref, l_out, ga, gb, ea, eb, sa, sb,
+                 x0, x1, p0, p1, s0, s1, w0, w1, g0, g1, l0, l1, e0, e1, scale0, scale1, in_sem, out_sem):
     copies = [
         pltpu.make_async_copy(d_ref.at[0, 0], g0, in_sem.at[0]),
         pltpu.make_async_copy(d_ref.at[1, 1], g1, in_sem.at[1]),
@@ -274,10 +279,31 @@
         c.start()
     for c in copies:
         c.wait()
-    factor_all((g0, g1), (x0, x1), (p0, p1), (s0, s1), (w0, w1), (l0, l1), (e0, e1), (scale0, scale1))
+    factor_steps(0, 2, (g0, g1), (x0, x1), (p0, p1), (s0, s1), (w0, w1), (l0, l1), (e0, e1), (scale0, scale1))
     outs = [
-        pltpu.make_async_copy(l0, l_out.at[0, 0], out_sem.at[0]),
-        pltpu.make_async_copy(l1, l_out.at[1, 0], out_sem.at[1]),
+        pltpu.make_async_copy(l_ref.at[:, 0:H], l_out.at[m, 0, :, 0:H], out_sem.at[m])
+        for m, l_ref in enumerate((l0, l1))
+    ]
+    for c in outs:
+        c.start()
+    for dst, src in ((ga, g0), (gb, g1)):
+        dst[...] = src[H:N, :]
+    for dst, src in ((ea, e0), (eb, e1), (sa, scale0), (sb, scale1)):
+        dst[...] = src[0:H, :]
+    for c in outs:
+        c.wait()
+
+
+def second_kernel(l_in, ga, gb, ea, eb, sa, sb, l_out, e0, e1, scale0, scale1, packed,
+                  x0, x1, p0, p1, s0, s1, w0, w1, g0, g1, l0, l1, out_sem):
+    for dst, src in ((g0, ga), (g1, gb)):
+        dst[H:N, :] = src[...]
+    for dst, src in ((e0, ea), (e1, eb), (scale0, sa), (scale1, sb)):
+        dst[0:H, :] = src[...]
+    factor_steps(2, 4, (g0, g1), (x0, x1), (p0, p1), (s0, s1), (w0, w1), (l0, l1), (e0, e1), (scale0, scale1))
+    outs = [
+        pltpu.make_async_copy(l_ref.at[:, H:N], l_out.at[m, 0, :, H:N], out_sem.at[m])
+        for m, l_ref in enumerate((l0, l1))
     ]
     for c in outs:
         c.start()
@@ -286,17 +312,27 @@
         c.wait()
 
 
-def factor_call(diag_blocks):
-    half = pltpu.VMEM((NB, 2 * NB), F32)
+STATE = (
+    shape((H, N), F32), shape((H, N), F32), shape((H, N), BF16), shape((H, N), BF16),
+    shape((H, NB), F32), shape((H, NB), F32),
+)
+COL = pltpu.VMEM((N, NB), F32)
+
+
+def first_call(diag_blocks):
     return call(
-        factor_kernel,
+        first_kernel, (shape((2, 1, N, N), F32),) + STATE, [ANY], (ANY,) + (VM,) * 6,
+        HALF + [WIDE] * 4 + [B16, B16, COL, COL, DMA2, DMA2], 30, 20,
+    )(diag_blocks)
+
+
+def second_call(*args):
+    return call(
+        second_kernel,
         (shape((2, 1, N, N), F32), shape((N, N), BF16), shape((N, N), BF16),
          shape((N, NB), F32), shape((N, NB), F32), shape((PACKED, NB), BF16)),
-        [ANY], (ANY, VM, VM, VM, VM, VM),
-        [WIDE, WIDE] + [half] * 6 + [pltpu.VMEM((NB, N), F32)] * 2 + [WIDE, WIDE]
-        + [pltpu.SemaphoreType.DMA((2,)), pltpu.SemaphoreType.DMA((2,))],
-        60, 20,
-    )(diag_blocks)
+        [ANY] + [VM] * 6, (ANY, VM, VM, VM, VM, VM), HALF + [WIDE] * 4 + [DMA2], 30, 20, {0: 0},
+    )(*args)
 
 
 def local_kernel(d_ref, h_ref, v_ref, e0, e1, scale0, scale1, to_right, to_below, sbuf, dbuf, link_out,
@@ -450,23 +486,24 @@
 
 def passed(value, down, right):
     rows, cols = lax.axis_size("row"), lax.axis_size("col")
-    if not right:
-        return lax.ppermute(value, "row", [(i, (i + down) % rows) for i in range(rows)])
-    if not down:
-        return lax.ppermute(value, "col", [(i, (i + right) % cols) for i in range(cols)])
-    pairs = [(r * cols + c, ((r + down) % rows) * cols + (c + right) % cols) for r in range(rows) for c in range(cols)]
+    pairs = [
+        (r * cols + c, ((r + down) % rows) * cols + (c + right) % cols)
+        for r in range(rows)
+        for c in range(cols)
+    ]
     return lax.ppermute(value, ("row", "col"), pairs)
 
 
 def on_device(diag_blocks, horizontal, vertical):
     pair = jnp.stack([horizontal[0, 0], vertical[0, 0]])
-    below = passed(pair, -1, 0)
     right = passed(pair, 0, -1)
     below0 = passed(horizontal[0, 1], -1, 1)
-    factor, e0, e1, scale0, scale1, packed = factor_call(diag_blocks)
-    below_inverse = passed(packed, -1, 0)
+    state = first_call(diag_blocks)
+    below = passed(right, -1, 1)
+    factor, e0, e1, scale0, scale1, packed = second_call(*state)
     right_inverse = passed(packed, 0, -1)
     to_right, to_below, schur, southeast, links = local_call(diag_blocks, horizontal, vertical, e0, e1, scale0, scale1)
+    below_inverse = passed(right_inverse, -1, 1)
     from_left = passed(to_right, 0, 1)
     from_above = passed(to_below, 1, 0)
     schur, southwest, links = across_call(

time: 77.6 us -> 93.4 us (1.20)
  waiting for transfers between devices: 23.9 us -> 36.9 us
  starting transfers between devices: 14.8 us -> 16.7 us
    ppermute x1 -> x7, waiting for transfers between devices: 8.51 us -> 36.9 us  [passed(): return lax.ppermute(value, ('row', 'col'), pairs)]
    ppermute x6 -> x0, waiting for transfers between devices: 15.3 us -> none  [the longest x3 8.6 us: passed(): lax.ppermute(value, 'row', [(i, (i + down) % rows) for i in range(rows)])]
    ppermute x1 -> x7, starting transfers between devices: 1.4 us -> 16.7 us  [passed(): return lax.ppermute(value, ('row', 'col'), pairs)]
    ppermute x6 -> x0, starting transfers between devices: 13.4 us -> none  [the longest x3 9.93 us: passed(): lax.ppermute(value, 'row', [(i, (i + down) % rows) for i in range(rows)])]
    pallas_call x1 -> x2, Pallas kernels: 23.7 us -> 24.6 us  [the longest x1 13.8 us: first_call(): call(first_kernel, (shape((2, 1, N, N), F32),) + STATE, [ANY], (ANY,) + (...]
  transfers between devices with their start and end apart: 7 -> 7, of which waited for: 5 -> 3; matrix products, arithmetic and copies ran while one was open for 0% -> 0% of each run, Pallas kernels for 43% -> 37%
where the time goes in v1:
time: 93.4 us; the launch traced here: 93.3 us
  waiting for transfers between devices  36.9 us (40%)
  Pallas kernels  36.2 us (39%)
  starting transfers between devices  16.7 us (18%)
  local copies, waits for them, and re-layouts  2.52 us (3%)
    ppermute x7, waiting for transfers between devices, passed(): return lax.ppermute(value, ('row', 'col'), pairs)  36.9 us
    ppermute x7, starting transfers between devices, passed(): return lax.ppermute(value, ('row', 'col'), pairs)  16.7 us
    pallas_call x1, Pallas kernels, first_call(): call(first_kernel, (shape((2, 1, N, N), F32),) + STATE, [ANY], (ANY,) + (...  13.8 us
    pallas_call x1, Pallas kernels, second_call(): call(second_kernel, (shape((2, 1, N, N), F32), shape((N, N), BF16), shape...  10.9 us
    pallas_call x1, Pallas kernels, local_call(): call(local_kernel, (shape((PACKED + N * N // NB, NB), BF16), shape((PACKE...  5.61 us
    pallas_call x1, Pallas kernels, across_call(): call(across_kernel, (shape((2, N, N), F32), shape((N, N), F32), shape((2,...  4.17 us
  transfers between devices with their start and end apart: 7, of which 3 were waited for; matrix products, arithmetic and copies ran while one was open for 0% of the time, Pallas kernels for 37%

profile of v1, /device:TPU:0, one launch (start us, length us, event | category | flops | bytes accessed | tf_op | source)
XLA Modules:
  0.0 93.3 jit_solution(1052575568065826029)
XLA Ops:
  0.6 1.1 %slice_bitcast_fusion.1 = bf16[1,512,512]{2,1,0:T(8,128)(2,1)S(1)} fusion(bf16[2,2,512,512]{3,2,1,0:T(8,128)(2,1)} %v_ref.3), kind=kLoop, calls=%fused_computation.2 | loop fusion | bytes 1048576 | tf_op jit(solution)/shard_map/stack;squeeze | solution.py:498
  1.7 0.0 copy-start.2
  1.7 1.4 %slice_bitcast_fusion = (bf16[512,512]{1,0:T(8,128)(2,1)S(1)}, bf16[1,512,512]{2,1,0:T(8,128)(2,1)S(1)}) fusion(bf16[2,2,512,512]{3,2,1,0:T(8,128)(2,1)} %h_ref.3), kind=kLoop, calls=%fused_computation.1 | loop fusion | bytes 2097152 | tf_op jit(solution)/shard_map/squeeze | solution.py:500
  3.1 0.1 pad_maximum_fusion
  3.3 3.6 %collective-permute-start.4 = (bf16[2,512,512]{2,1,0:T(8,128)(2,1)S(1)}, bf16[2,512,512]{2,1,0:T(8,128)(2,1)S(1)}, u32[]{:S(2)}, u32[]{:S(2)}) collective-permute-start(bf16[2,512,512]{2,1,0:T(8,128)(2,1)S(1)} %pad_maximum_fusion), channel_id=1, source_target_pairs={{0,15},{1,0},{2,1},{3,2},{4,3},{5,4},{6,5},{7,6},{8,7},{9,8},{10,9... | collective-permute-start | bytes 3145736 | tf_op jit(solution)/shard_map/ppermute | solution.py:494
  6.8 13.8 %shard_map.58 = (f32[2,1,512,512]{3,2,1,0:T(8,128)}, f32[256,512]{1,0:T(8,128)S(1)}, f32[256,512]{1,0:T(8,128)S(1)}, bf16[256,512]{1,0:T(8,128)(2,1)S(1)}, bf16[...) custom-call(f32[2,2,512,512]{3,2,1,0:T(8,128)S(1)} %copy-done.2), custom_call_target="tpu_custom_call" | custom-call | flops 30000001024 | bytes 4194304 | tf_op jit(solution)/shard_map/pallas_call | solution.py:323
  20.6 0.0 copy-start
  20.6 0.0 copy-start.1
  20.6 10.9 %shard_map.59 = (f32[2,1,512,512]{3,2,1,0:T(8,128)}, bf16[512,512]{1,0:T(8,128)(2,1)S(1)}, bf16[512,512]{1,0:T(8,128)(2,1)S(1)}, f32[512,128]{1,0:T(8,128)S(1)},...) custom-call(f32[2,1,512,512]{3,2,1,0:T(8,128)} %get-tuple-element.26.l_in, ...), custom_call_target="tpu_custom_call", output_to_operand_aliasing={{0}: (0, {})} | custom-call | flops 30000001024 | bytes 4194304 | tf_op jit(solution)/shard_map/pallas_call | solution.py:330
  31.5 1.0 %collective-permute-start.2 = (bf16[1040,128]{1,0:T(8,128)(2,1)S(1)}, bf16[1040,128]{1,0:T(8,128)(2,1)S(1)}, u32[]{:S(2)}, u32[]{:S(2)}) collective-permute-start(bf16[1040,128]{1,0:T(8,128)(2,1)S(1)} %get-tuple-element.40), channel_id=1, source_target_pairs={{0,15},{1,0},{2,1},{3,2},{4,3},{5,4},{6,5},{7,6},{8,7},{9,8},{10,9... | collective-permute-start | bytes 798728 | tf_op jit(solution)/shard_map/ppermute | solution.py:494
  32.4 5.4 %collective-permute-start.6 = (bf16[512,512]{1,0:T(8,128)(2,1)S(1)}, bf16[512,512]{1,0:T(8,128)(2,1)S(1)}, u32[]{:S(2)}, u32[]{:S(2)}) collective-permute-start(bf16[512,512]{1,0:T(8,128)(2,1)S(1)} %get-tuple-element.49), channel_id=1, source_target_pairs={{0,113},{1,114},{2,115},{3,116},{4,117},{5,118},{6,119},{7,120},{8... | collective-permute-start | bytes 1572872 | tf_op jit(solution)/shard_map/ppermute | solution.py:494
  37.9 0.0 collective-permute-done.2.rpack
  37.9 3.0 %collective-permute-start.3 = (bf16[1040,128]{1,0:T(8,128)(2,1)S(1)}, bf16[1040,128]{1,0:T(8,128)(2,1)S(1)}, u32[]{:S(2)}, u32[]{:S(2)}) collective-permute-start(bf16[1040,128]{1,0:T(8,128)(2,1)S(1)} %collective-permute-done.2.rpack), channel_id=1, source_target_pairs={{0,113},{1,114},{2,115},{3,116},{4,117},{5,118},{6,119},{7,120},{8... | collective-permute-start | bytes 798728 | tf_op jit(solution)/shard_map/ppermute | solution.py:494
  40.8 0.0 collective-permute-done.4.rc
  40.8 0.0 collective-permute-start.5
  40.9 5.6 %shard_map.60 = (bf16[3088,128]{1,0:T(8,128)(2,1)S(1)}, bf16[1040,128]{1,0:T(8,128)(2,1)S(1)}, f32[2,512,512]{2,1,0:T(8,128)S(1)}, f32[2,512,512]{2,1,0:T(8,128)S(1)}, bf16[2,1,4,512,512]{4,3,2,1,0:T(8,128)(2,1)}) custom-call(f32[2,2,512,512]{3,2,1,0:T(8,128)S(1)} %copy-done.2, bf16[2,2,512,512]{3,2,1,0:T(8,128)(2,1)S(1)} %copy-done, ...), custom_call_target="tpu_custom_call" | custom-call | flops 12000000000 | bytes 4194304 | tf_op jit(solution)/shard_map/pallas_call | solution.py:387
  46.5 1.9 %collective-permute-start.1 = (bf16[1040,128]{1,0:T(8,128)(2,1)S(1)}, bf16[1040,128]{1,0:T(8,128)(2,1)S(1)}, u32[]{:S(2)}, u32[]{:S(2)}) collective-permute-start(bf16[1040,128]{1,0:T(8,128)(2,1)S(1)} %get-tuple-element.39), channel_id=1, source_target_pairs={{0,16},{1,17},{2,18},{3,19},{4,20},{5,21},{6,22},{7,23},{8,24},{9,... | collective-permute-start | bytes 798728 | tf_op jit(solution)/shard_map/ppermute | solution.py:494
  48.4 1.8 %collective-permute-start = (bf16[3088,128]{1,0:T(8,128)(2,1)S(1)}, bf16[3088,128]{1,0:T(8,128)(2,1)S(1)}, u32[]{:S(2)}, u32[]{:S(2)}) collective-permute-start(bf16[3088,128]{1,0:T(8,128)(2,1)S(1)} %get-tuple-element.38), channel_id=1, source_target_pairs={{0,1},{1,2},{2,3},{3,4},{4,5},{5,6},{6,7},{7,8},{8,9},{9,10},{10,1... | collective-permute-start | bytes 2371592 | tf_op jit(solution)/shard_map/ppermute | solution.py:494
  50.2 19.6 %collective-permute-done.6.bc0 = bf16[512,512]{1,0:T(8,128)(2,1)S(1)} collective-permute-done((bf16[512,512]{1,0:T(8,128)(2,1)S(1)}, bf16[512,512]{1,0:T(8,128)(2,1)S(1)}, u32[]{:S(2)}, u32[]{:S(2)}) %collective-permute-start.6) | collective-permute-done | bytes 524320 | tf_op jit(solution)/shard_map/ppermute | solution.py:494
  69.8 4.4 %collective-permute-done.3.bpack = bf16[1040,128]{1,0:T(8,128)(2,1)S(1)} collective-permute-done((bf16[1040,128]{1,0:T(8,128)(2,1)S(1)}, bf16[1040,128]{1,0:T(8,128)(2,1)S(1)}, u32[]{:S(2)}, u32[]{:S(2)}) %collective-permute-start.3) | collective-permute-done | bytes 266272 | tf_op jit(solution)/shard_map/ppermute | solution.py:494
  74.3 12.8 %collective-permute-done.5.bc = bf16[2,512,512]{2,1,0:T(8,128)(2,1)S(1)} collective-permute-done((bf16[2,512,512]{2,1,0:T(8,128)(2,1)S(1)}, bf16[2,512,512]{2,1,0:T(8,128)(2,1)S(1)}, u32[]{:S(2)}, u32[]{:S(2)}) %collective-permute-start.5) | collective-permute-done | bytes 1048608 | tf_op jit(solution)/shard_map/ppermute | solution.py:494
  87.1 4.2 %shard_map.61 = (f32[2,512,512]{2,1,0:T(8,128)S(1)}, f32[512,512]{1,0:T(8,128)S(1)}, bf16[2,1,4,512,512]{4,3,2,1,0:T(8,128)(2,1)}) custom-call(bf16[2,2,512,512]{3,2,1,0:T(8,128)(2,1)S(1)} %copy-done, bf16[2,2,512,512]{3,2,1,0:T(8,128)(2,1)S(1)} %copy-done.1, bf16[1040,128]{1,0:T(8,128)(2,1)S(1)} %collective-permute-done.2.rpack, ...), custom_call_target="tpu_custom_call", output_to_operand_aliasing={{2}: (9, {})} | custom-call | flops 10000000000 | bytes 4194304 | tf_op jit(solution)/shard_map/pallas_call | solution.py:439
  91.2 0.0 collective-permute-done.1.from_above
  91.3 1.9 %shard_map.62 = (f32[2,1,512,512]{3,2,1,0:T(8,128)}, bf16[2,1,4,512,512]{4,3,2,1,0:T(8,128)(2,1)}) custom-call(bf16[3088,128]{1,0:T(8,128)(2,1)S(1)} %collective-permute-done.from_left, bf16[1040,128]{1,0:T(8,128)(2,1)S(1)} %collective-permute-done.1.from_above, f32[2,512,512]{2,1,0:T(8,128)S(1)} %get-tuple-element.44.schur_in, ...), custom_call_target="tpu_custom_call", output_to_operand_aliasing={{1}: (4, {})} | custom-call | flops 2000000000 | bytes 4194304 | tf_op jit(solution)/shard_map/pallas_call | solution.py:478
  (4 shorter events, 0.0 us)
Async XLA Ops:
  1.7 5.1 %copy-start.2 = (f32[2,2,512,512]{3,2,1,0:T(8,128)S(1)}, f32[2,2,512,512]{3,2,1,0:T(8,128)}, u32[]{:S(2)}) copy-start(f32[2,2,512,512]{3,2,1,0:T(8,128)} %d_ref.3) | copy-start | bytes 12582916
  3.3 37.6 %collective-permute-start.4 = (bf16[2,512,512]{2,1,0:T(8,128)(2,1)S(1)}, bf16[2,512,512]{2,1,0:T(8,128)(2,1)S(1)}, u32[]{:S(2)}, u32[]{:S(2)}) collective-permute-start(bf16[2,512,512]{2,1,0:T(8,128)(2,1)S(1)} %pad_maximum_fusion), channel_id=1, source_target_pairs={{0,15},{1,0},{2,1},{3,2},{4,3},{5,4},{6,5},{7,6},{8,7},{9,8},{10,9... | collective-permute-start | bytes 3145736 | tf_op jit(solution)/shard_map/ppermute | solution.py:494
  20.6 20.3 %copy-start = (bf16[2,2,512,512]{3,2,1,0:T(8,128)(2,1)S(1)}, bf16[2,2,512,512]{3,2,1,0:T(8,128)(2,1)}, u32[]{:S(2)}) copy-start(bf16[2,2,512,512]{3,2,1,0:T(8,128)(2,1)} %h_ref.3) | copy-start | bytes 6291460
  20.6 20.3 %copy-start.1 = (bf16[2,2,512,512]{3,2,1,0:T(8,128)(2,1)S(1)}, bf16[2,2,512,512]{3,2,1,0:T(8,128)(2,1)}, u32[]{:S(2)}) copy-start(bf16[2,2,512,512]{3,2,1,0:T(8,128)(2,1)} %v_ref.3) | copy-start | bytes 6291460
  31.5 6.4 %collective-permute-start.2 = (bf16[1040,128]{1,0:T(8,128)(2,1)S(1)}, bf16[1040,128]{1,0:T(8,128)(2,1)S(1)}, u32[]{:S(2)}, u32[]{:S(2)}) collective-permute-start(bf16[1040,128]{1,0:T(8,128)(2,1)S(1)} %get-tuple-element.40), channel_id=1, source_target_pairs={{0,15},{1,0},{2,1},{3,2},{4,3},{5,4},{6,5},{7,6},{8,7},{9,8},{10,9... | collective-permute-start | bytes 798728 | tf_op jit(solution)/shard_map/ppermute | solution.py:494
  32.4 37.4 %collective-permute-start.6 = (bf16[512,512]{1,0:T(8,128)(2,1)S(1)}, bf16[512,512]{1,0:T(8,128)(2,1)S(1)}, u32[]{:S(2)}, u32[]{:S(2)}) collective-permute-start(bf16[512,512]{1,0:T(8,128)(2,1)S(1)} %get-tuple-element.49), channel_id=1, source_target_pairs={{0,113},{1,114},{2,115},{3,116},{4,117},{5,118},{6,119},{7,120},{8... | collective-permute-start | bytes 1572872 | tf_op jit(solution)/shard_map/ppermute | solution.py:494
  37.9 36.4 %collective-permute-start.3 = (bf16[1040,128]{1,0:T(8,128)(2,1)S(1)}, bf16[1040,128]{1,0:T(8,128)(2,1)S(1)}, u32[]{:S(2)}, u32[]{:S(2)}) collective-permute-start(bf16[1040,128]{1,0:T(8,128)(2,1)S(1)} %collective-permute-done.2.rpack), channel_id=1, source_target_pairs={{0,113},{1,114},{2,115},{3,116},{4,117},{5,118},{6,119},{7,120},{8... | collective-permute-start | bytes 798728 | tf_op jit(solution)/shard_map/ppermute | solution.py:494
  40.8 46.2 %collective-permute-start.5 = (bf16[2,512,512]{2,1,0:T(8,128)(2,1)S(1)}, bf16[2,512,512]{2,1,0:T(8,128)(2,1)S(1)}, u32[]{:S(2)}, u32[]{:S(2)}) collective-permute-start(bf16[2,512,512]{2,1,0:T(8,128)(2,1)S(1)} %collective-permute-done.4.rc), channel_id=1, source_target_pairs={{0,113},{1,114},{2,115},{3,116},{4,117},{5,118},{6,119},{7,120},{8... | collective-permute-start | bytes 3145736 | tf_op jit(solution)/shard_map/ppermute | solution.py:494
  46.5 44.7 %collective-permute-start.1 = (bf16[1040,128]{1,0:T(8,128)(2,1)S(1)}, bf16[1040,128]{1,0:T(8,128)(2,1)S(1)}, u32[]{:S(2)}, u32[]{:S(2)}) collective-permute-start(bf16[1040,128]{1,0:T(8,128)(2,1)S(1)} %get-tuple-element.39), channel_id=1, source_target_pairs={{0,16},{1,17},{2,18},{3,19},{4,20},{5,21},{6,22},{7,23},{8,24},{9,... | collective-permute-start | bytes 798728 | tf_op jit(solution)/shard_map/ppermute | solution.py:494
  48.4 42.8 %collective-permute-start = (bf16[3088,128]{1,0:T(8,128)(2,1)S(1)}, bf16[3088,128]{1,0:T(8,128)(2,1)S(1)}, u32[]{:S(2)}, u32[]{:S(2)}) collective-permute-start(bf16[3088,128]{1,0:T(8,128)(2,1)S(1)} %get-tuple-element.38), channel_id=1, source_target_pairs={{0,1},{1,2},{2,3},{3,4},{4,5},{5,6},{6,7},{7,8},{8,9},{9,10},{10,1... | collective-permute-start | bytes 2371592 | tf_op jit(solution)/shard_map/ppermute | solution.py:494

commit v2 on v0

--- a/solution.py
+++ b/solution.py
@@ -86,7 +86,7 @@
     return jnp.concatenate([x] * (N // NB), 1)
 
 
-def factor_all(g_refs, x_refs, p_refs, s_refs, w_refs, l_refs, e_refs, scale_refs):
+def factor_steps(first, last, g_refs, x_refs, p_refs, s_refs, w_refs, l_refs, e_refs, scale_refs):
     r_i = lax.broadcasted_iota(jnp.int32, (NB, NB), 0)
     c_i = lax.broadcasted_iota(jnp.int32, (NB, NB), 1)
     wide = lax.broadcasted_iota(jnp.int32, (NB, N), 1)
@@ -111,7 +111,7 @@
             unit = w_ref[...] * tiled(s_ref[:, NB : 2 * NB])
             e_refs[m][here, :] = jnp.where(wide < base + NB, unit, 0.0).astype(BF16)
             scale_refs[m][here, :] = s_ref[:, 0:NB]
-        for p in range(1, N // NB):
+        for p in range(first + 1, N // NB):
             rows = slice(p * NB, (p + 1) * NB)
 
             @pl.when(p > o)
@@ -124,7 +124,7 @@
 
         return carry
 
-    lax.fori_loop(0, N // NB, outer, 0)
+    lax.fori_loop(first, last, outer, 0)
 
 
 LOWER = [(r, c) for r in range(N // NB) for c in range(r)]
@@ -264,56 +264,80 @@
     )
 
 
-def factor_kernel(d_ref, l_out, e0, e1, scale0, scale1, packed,
-                  g0, g1, x0, x1, p0, p1, s0, s1, w0, w1, l0, l1, in_sem, out_sem):
+WORK = [pltpu.VMEM((NB, 2 * NB), F32)] * 6 + [pltpu.VMEM((NB, N), F32)] * 2 + [WIDE] * 4
+DMA2 = pltpu.SemaphoreType.DMA((2,))
+ENDS = (shape((N, N), BF16), shape((N, N), BF16), shape((N, NB), F32), shape((N, NB), F32))
+
+
+def factor_part(first, last):
+    lo, hi = first * NB, last * NB
+    ending = hi == N
+
+    def kernel(*refs):
+        refs = list(refs)
+        take = lambda n: [refs.pop(0) for _ in range(n)]
+        source = take(1)[0]
+        before = take(6) if first else ()
+        l_out = take(1)[0]
+        after = take(5) if ending else take(6)
+        x0, x1, p0, p1, s0, s1, w0, w1, g0, g1, l0, l1 = take(12)
+        state = tuple(after[:4]) if ending else tuple(take(4))
+        in_sem, out_sem = take(2)
+        if first:
+            for dst, src in zip((g0, g1), before):
+                dst[lo:N, :] = src[...]
+            for dst, src in zip(state, before[2:]):
+                dst[0:lo, :] = src[...]
+        else:
+            copies = [
+                pltpu.make_async_copy(source.at[m, m], g_ref, in_sem.at[m])
+                for m, g_ref in enumerate((g0, g1))
+            ]
+            for c in copies:
+                c.start()
+            for c in copies:
+                c.wait()
+        factor_steps(first, last, (g0, g1), (x0, x1), (p0, p1), (s0, s1), (w0, w1), (l0, l1), state[:2], state[2:])
+        outs = [
+            pltpu.make_async_copy(l_ref.at[:, lo:hi], l_out.at[m, 0, :, lo:hi], out_sem.at[m])
+            for m, l_ref in enumerate((l0, l1))
+        ]
+        for c in outs:
+            c.start()
+        if ending:
+            pack_unit(state[0], state[2], after[4])
+        else:
+            for dst, src in zip(after, (g0, g1)):
+                dst[...] = src[hi:N, :]
+            for dst, src in zip(after[2:], state):
+                dst[...] = src[0:hi, :]
+        for c in outs:
+            c.wait()
+
+    if ending:
+        outs = ENDS + (shape((PACKED, NB), BF16),)
+        scratch = []
+    else:
+        outs = (shape((N - hi, N), F32),) * 2 + (shape((hi, N), BF16),) * 2 + (shape((hi, NB), F32),) * 2
+        scratch = [B16, B16, pltpu.VMEM((N, NB), F32), pltpu.VMEM((N, NB), F32)]
+    return call(
+        kernel, (shape((2, 1, N, N), F32),) + outs,
+        [ANY] + [VM] * (6 if first else 0), (ANY,) + (VM,) * len(outs),
+        WORK + scratch + [DMA2, DMA2], 15 * (last - first), 13, {0: 0} if first else None,
+    )
+
+
+def products_kernel(h_ref, v_ref, e1, scale1, to_right, to_below, y2, y3, c2, c3, in_sem):
     copies = [
-        pltpu.make_async_copy(d_ref.at[0, 0], g0, in_sem.at[0]),
-        pltpu.make_async_copy(d_ref.at[1, 1], g1, in_sem.at[1]),
+        pltpu.make_async_copy(h_ref.at[1, 1], c2, in_sem.at[0]),
+        pltpu.make_async_copy(v_ref.at[1, 1], c3, in_sem.at[1]),
     ]
     for c in copies:
         c.start()
     for c in copies:
         c.wait()
-    factor_all((g0, g1), (x0, x1), (p0, p1), (s0, s1), (w0, w1), (l0, l1), (e0, e1), (scale0, scale1))
-    outs = [
-        pltpu.make_async_copy(l0, l_out.at[0, 0], out_sem.at[0]),
-        pltpu.make_async_copy(l1, l_out.at[1, 0], out_sem.at[1]),
-    ]
-    for c in outs:
-        c.start()
-    pack_unit(e0, scale0, packed)
-    for c in outs:
-        c.wait()
-
-
-def factor_call(diag_blocks):
-    half = pltpu.VMEM((NB, 2 * NB), F32)
-    return call(
-        factor_kernel,
-        (shape((2, 1, N, N), F32), shape((N, N), BF16), shape((N, N), BF16),
-         shape((N, NB), F32), shape((N, NB), F32), shape((PACKED, NB), BF16)),
-        [ANY], (ANY, VM, VM, VM, VM, VM),
-        [WIDE, WIDE] + [half] * 6 + [pltpu.VMEM((NB, N), F32)] * 2 + [WIDE, WIDE]
-        + [pltpu.SemaphoreType.DMA((2,)), pltpu.SemaphoreType.DMA((2,))],
-        60, 20,
-    )(diag_blocks)
-
-
-def local_kernel(d_ref, h_ref, v_ref, e0, e1, scale0, scale1, to_right, to_below, sbuf, dbuf, link_out,
-                 hh, hv, y0, y1, y2, y3, z2, z3, lbuf, row1, in_sem, out_sem):
-    copies = [
-        pltpu.make_async_copy(h_ref, hh, in_sem.at[0]),
-        pltpu.make_async_copy(v_ref, hv, in_sem.at[1]),
-        pltpu.make_async_copy(d_ref.at[0, 1], sbuf.at[0], in_sem.at[2]),
-        pltpu.make_async_copy(d_ref.at[1, 0], sbuf.at[1], in_sem.at[3]),
-    ]
-    for c in copies:
-        c.start()
-    for c in copies[:2]:
-        c.wait()
-    scale_row(scale1, row1)
-    solve_n(e1, scale1, hh.at[1, 1], y2)
-    solve_n(e1, scale1, hv.at[1, 1], y3)
+    solve_n(e1, scale1, c2, y2)
+    solve_n(e1, scale1, c3, y3)
     t2 = y2[...].T
     pack_symmetric(dot(t2, y2[...]), to_right)
     side = dot(t2, y3[...])
@@ -321,26 +345,50 @@
         for c in range(N // NB):
             to_right[at(PACKED, 4 * r + c), :] = block(side, r, c).astype(BF16)
     pack_symmetric(dot(y3[...].T, y3[...]), to_below)
-    solve_t(e1, row1, hh.at[1, 0], y0)
-    solve_t(e1, row1, hv.at[0, 1], y1)
-    solve_n(e0, scale0, hh.at[0, 0], z2)
-    solve_n(e0, scale0, hv.at[0, 0], z3)
-    u2 = z2[...].T
-    for c in copies[2:]:
+
+
+def products_call(*args):
+    return call(
+        products_kernel,
+        (shape((PACKED + N * N // NB, NB), BF16), shape((PACKED, NB), BF16), shape((N, N), BF16),
+         shape((N, N), BF16)),
+        [ANY] * 2 + [VM] * 2, (VM,) * 4, [B16, B16, DMA2], 4, 8,
+    )(*args)
+
+
+def local_kernel(d_ref, h_ref, v_ref, e0, e1, scale0, scale1, y2, y3, sbuf, dbuf, link_out,
+                 c0, c1, f2, f3, y0, y1, z2, z3, lbuf, row1, in_sem, out_sem):
+    copies = [
+        pltpu.make_async_copy(src, dst, in_sem.at[k])
+        for k, (src, dst) in enumerate(
+            (
+                (h_ref.at[1, 0], c0),
+                (v_ref.at[0, 1], c1),
+                (h_ref.at[0, 0], f2),
+                (v_ref.at[0, 0], f3),
+                (d_ref.at[0, 1], sbuf.at[0]),
+                (d_ref.at[1, 0], sbuf.at[1]),
+            )
+        )
+    ]
+    for c in copies:
+        c.start()
+    scale_row(scale1, row1)
+    for c in copies[:4]:
         c.wait()
     outs = []
-
-    def link(slot, row, which, value):
-        lbuf[slot] = (-value).astype(BF16)
-        copy = pltpu.make_async_copy(lbuf.at[slot], link_out.at[row, 0, which], out_sem.at[slot])
-        copy.start()
-        outs.append(copy)
-
-    link(0, 0, 1, dot(y1[...], y3[...]))
-    link(1, 0, 3, dot(u2, z3[...]) + dot(y1[...], y0[...], 1, 1))
-    link(2, 1, 0, dot(y0[...], y2[...]))
+    solve_t(e1, row1, c1, y1)
+    put_link(outs, lbuf, link_out, out_sem, 0, 1, dot(y1[...], y3[...]))
+    solve_t(e1, row1, c0, y0)
+    put_link(outs, lbuf, link_out, out_sem, 1, 0, dot(y0[...], y2[...]))
+    solve_n(e0, scale0, f2, z2)
+    solve_n(e0, scale0, f3, z3)
+    u2 = z2[...].T
+    put_link(outs, lbuf, link_out, out_sem, 0, 3, dot(u2, z3[...]) + dot(y1[...], y0[...], 1, 1))
     dbuf[0] = dot(y1[...], y2[...])
     dbuf[1] = dot(y0[...], y3[...])
+    for c in copies[4:]:
+        c.wait()
     sbuf[0] = sbuf[0] - (dot(u2, z2[...]) + dot(y1[...], y1[...], 1, 1))
     sbuf[1] = sbuf[1] - (dot(z3[...].T, z3[...]) + dot(y0[...], y0[...], 1, 1))
     for c in outs:
@@ -350,130 +398,132 @@
 def local_call(*args):
     return call(
         local_kernel,
-        (shape((PACKED + N * N // NB, NB), BF16), shape((PACKED, NB), BF16), shape((2, N, N), F32),
-         shape((2, N, N), F32), shape((2, 1, 4, N, N), BF16)),
-        [ANY] * 3 + [VM] * 4, (VM, VM, VM, VM, ANY),
-        [pltpu.VMEM((2, 2, N, N), BF16)] * 2 + [B16] * 6
-        + [pltpu.VMEM((3, N, N), BF16), pltpu.VMEM((8, N), F32)]
-        + [pltpu.SemaphoreType.DMA((4,)), pltpu.SemaphoreType.DMA((3,))],
-        12, 28,
+        (shape((2, N, N), F32), shape((2, N, N), F32), shape((2, 1, 4, N, N), BF16)),
+        [ANY] * 3 + [VM] * 6, (VM, VM, ANY),
+        [B16] * 8 + [pltpu.VMEM((3, N, N), BF16), pltpu.VMEM((8, N), F32)]
+        + [pltpu.SemaphoreType.DMA((6,)), pltpu.SemaphoreType.DMA((3,))],
+        9, 16,
     )(*args)
 
 
-def across_kernel(h_ref, v_ref, rpack, bpack, rc, bc, bc0, se, schur_in, link_in, schur_out, sw, link_out,
-                  inv_a, inv_b, c0, c1, ra0, r2, r3, b0, b1, b2, b3, scale_a, scale_b, row_a, row_b,
-                  lbuf, in_sem, sem):
-    loads = [
-        pltpu.make_async_copy(h_ref.at[0, 1], c0, in_sem.at[0]),
-        pltpu.make_async_copy(v_ref.at[1, 0], c1, in_sem.at[1]),
-    ]
-    for c in loads:
-        c.start()
-    unpack_unit(rpack, inv_a, scale_a, row_a)
-    unpack_unit(bpack, inv_b, scale_b, row_b)
-    for c in loads:
-        c.wait()
+def put_link(outs, buffer, out, sem, row, which, value):
+    slot = len(outs)
+    buffer[slot] = (-value).astype(BF16)
+    copy = pltpu.make_async_copy(buffer.at[slot], out.at[row, 0, which], sem.at[slot])
+    copy.start()
+    outs.append(copy)
+
+
+def right_kernel(h_ref, rpack, rc, se, schur_in, link_in, schur0, link_out,
+                 inv, c0, w0, w2, w3, scale, row, lbuf, in_sem, sem):
+    load = pltpu.make_async_copy(h_ref.at[0, 1], c0, in_sem)
+    load.start()
+    unpack_unit(rpack, inv, scale, row)
+    load.wait()
     outs = []
-
-    def link(slot, row, which, value):
-        lbuf[slot] = (-value).astype(BF16)
-        copy = pltpu.make_async_copy(lbuf.at[slot], link_out.at[row, 0, which], sem.at[slot])
-        copy.start()
-        outs.append(copy)
-
-    solve_t(inv_a, row_a, c0, ra0)
-    solve_n(inv_a, scale_a, rc.at[0], r2)
-    solve_n(inv_a, scale_a, rc.at[1], r3)
-    link(0, 0, 0, dot(ra0[...], r2[...]))
-    link(1, 0, 2, dot(ra0[...], r3[...]) + se[0])
-    solve_t(inv_b, row_b, c1, b1)
-    solve_n(inv_b, scale_b, bc.at[1], b3)
-    link(2, 1, 1, dot(b1[...], b3[...]))
-    solve_n(inv_b, scale_b, bc.at[0], b2)
-    link(3, 1, 2, dot(b1[...], b2[...]) + se[1])
-    solve_t(inv_b, row_b, bc0, b0)
-    schur_out[0] = schur_in[0] - dot(ra0[...], ra0[...], 1, 1)
-    schur_out[1] = schur_in[1] - dot(b1[...], b1[...], 1, 1)
-    sw[...] = dot(b1[...], b0[...], 1, 1)
+    solve_t(inv, row, c0, w0)
+    solve_n(inv, scale, rc.at[0], w2)
+    put_link(outs, lbuf, link_out, sem, 0, 0, dot(w0[...], w2[...]))
+    solve_n(inv, scale, rc.at[1], w3)
+    put_link(outs, lbuf, link_out, sem, 0, 2, dot(w0[...], w3[...]) + se[0])
+    schur0[...] = schur_in[0] - dot(w0[...], w0[...], 1, 1)
     for c in outs:
         c.wait()
 
 
-def across_call(*args):
+def right_call(*args):
     return call(
-        across_kernel,
-        (shape((2, N, N), F32), shape((N, N), F32), shape((2, 1, 4, N, N), BF16)),
-        [ANY] * 2 + [VM] * 7 + [ANY], (VM, VM, ANY),
-        [B16] * 11 + [pltpu.VMEM((N, NB), F32)] * 2 + [pltpu.VMEM((8, N), F32)] * 2
-        + [pltpu.VMEM((4, N, N), BF16), pltpu.SemaphoreType.DMA((2,)), pltpu.SemaphoreType.DMA((4,))],
-        10, 30, {9: 2},
+        right_kernel, (shape((N, N), F32), shape((2, 1, 4, N, N), BF16)),
+        [ANY] + [VM] * 4 + [ANY], (VM, ANY),
+        [B16] * 5 + [pltpu.VMEM((N, NB), F32), pltpu.VMEM((8, N), F32), pltpu.VMEM((2, N, N), BF16)]
+        + [pltpu.SemaphoreType.DMA, DMA2],
+        5, 10, {5: 1},
     )(*args)
 
 
-def last_kernel(from_left, from_above, schur_in, sw, link_in, schur_out, link_out, sbuf, lbuf, sem):
-    lbuf[...] = jnp.concatenate(
+def sides_kernel(from_left, from_above, schur0, schur_in, schur_out, schur1, sbuf, sem):
+    sbuf[...] = schur0[...]
+    add_symmetric(from_above, sbuf)
+    copy = pltpu.make_async_copy(sbuf, schur_out.at[0, 0], sem)
+    copy.start()
+    schur1[...] = schur_in[1]
+    add_symmetric(from_left, schur1)
+    copy.wait()
+
+
+def sides_call(*args):
+    return call(
+        sides_kernel, (shape((2, 1, N, N), F32), shape((N, N), F32)),
+        [VM] * 4, (ANY, VM), [WIDE, pltpu.SemaphoreType.DMA], 1, 6,
+    )(*args)
+
+
+def below_kernel(v_ref, bpack, bc, bc0, se, from_left, schur1, schur_in, link_in, schur_out, link_out,
+                 inv, c1, w0, w1, w2, w3, scale, row, lbuf, sbuf, in_sem, sem):
+    load = pltpu.make_async_copy(v_ref.at[1, 0], c1, in_sem)
+    load.start()
+    unpack_unit(bpack, inv, scale, row)
+    load.wait()
+    outs = []
+    solve_t(inv, row, c1, w1)
+    sbuf[...] = schur1[...] - dot(w1[...], w1[...], 1, 1)
+    copy = pltpu.make_async_copy(sbuf, schur_out.at[1, 0], sem.at[3])
+    copy.start()
+    solve_n(inv, scale, bc.at[1], w3)
+    put_link(outs, lbuf, link_out, sem, 1, 1, dot(w1[...], w3[...]))
+    solve_n(inv, scale, bc.at[0], w2)
+    put_link(outs, lbuf, link_out, sem, 1, 2, dot(w1[...], w2[...]) + se[1])
+    solve_t(inv, row, bc0, w0)
+    side = jnp.concatenate(
         [
-            jnp.concatenate(
-                [
-                    (-(block(sw, r, c) + from_left[at(PACKED, 4 * r + c), :].astype(F32))).astype(BF16)
-                    for c in range(N // NB)
-                ],
-                1,
-            )
+            jnp.concatenate([from_left[at(PACKED, 4 * r + c), :] for c in range(N // NB)], 1)
             for r in range(N // NB)
         ],
         0,
     )
-    outs = [
-        pltpu.make_async_copy(lbuf, link_out.at[1, 0, 3], sem.at[0]),
-        pltpu.make_async_copy(sbuf.at[0], schur_out.at[0, 0], sem.at[1]),
-        pltpu.make_async_copy(sbuf.at[1], schur_out.at[1, 0], sem.at[2]),
-    ]
-    outs[0].start()
-    for m, src in enumerate((from_above, from_left)):
-        sbuf[m] = schur_in[m]
-        add_symmetric(src, sbuf.at[m])
-        outs[1 + m].start()
-    for c in outs:
+    put_link(outs, lbuf, link_out, sem, 1, 3, dot(w1[...], w0[...], 1, 1) + side.astype(F32))
+    for c in outs + [copy]:
         c.wait()
 
 
-def last_call(*args):
+def below_call(*args):
     return call(
-        last_kernel,
-        (shape((2, 1, N, N), F32), shape((2, 1, 4, N, N), BF16)),
-        [VM] * 4 + [ANY], (ANY, ANY),
-        [pltpu.VMEM((2, N, N), F32), B16, pltpu.SemaphoreType.DMA((3,))],
-        2, 16, {4: 1},
+        below_kernel, (shape((2, 1, N, N), F32), shape((2, 1, 4, N, N), BF16)),
+        [ANY] + [VM] * 6 + [ANY, ANY], (ANY, ANY),
+        [B16] * 6 + [pltpu.VMEM((N, NB), F32), pltpu.VMEM((8, N), F32), pltpu.VMEM((3, N, N), BF16), WIDE]
+        + [pltpu.SemaphoreType.DMA, pltpu.SemaphoreType.DMA((4,))],
+        6, 12, {7: 0, 8: 1},
     )(*args)
 
 
 def passed(value, down, right):
     rows, cols = lax.axis_size("row"), lax.axis_size("col")
-    if not right:
-        return lax.ppermute(value, "row", [(i, (i + down) % rows) for i in range(rows)])
-    if not down:
-        return lax.ppermute(value, "col", [(i, (i + right) % cols) for i in range(cols)])
-    pairs = [(r * cols + c, ((r + down) % rows) * cols + (c + right) % cols) for r in range(rows) for c in range(cols)]
+    pairs = [
+        (r * cols + c, ((r + down) % rows) * cols + (c + right) % cols)
+        for r in range(rows)
+        for c in range(cols)
+    ]
     return lax.ppermute(value, ("row", "col"), pairs)
 
 
 def on_device(diag_blocks, horizontal, vertical):
     pair = jnp.stack([horizontal[0, 0], vertical[0, 0]])
-    below = passed(pair, -1, 0)
     right = passed(pair, 0, -1)
     below0 = passed(horizontal[0, 1], -1, 1)
-    factor, e0, e1, scale0, scale1, packed = factor_call(diag_blocks)
-    below_inverse = passed(packed, -1, 0)
+    state = factor_part(0, 2)(diag_blocks)
+    below = passed(right, -1, 1)
+    factor, e0, e1, scale0, scale1, packed = factor_part(2, 4)(*state)
     right_inverse = passed(packed, 0, -1)
-    to_right, to_below, schur, southeast, links = local_call(diag_blocks, horizontal, vertical, e0, e1, scale0, scale1)
+    to_right, to_below, y2, y3 = products_call(horizontal, vertical, e1, scale1)
     from_left = passed(to_right, 0, 1)
     from_above = passed(to_below, 1, 0)
-    schur, southwest, links = across_call(
-        horizontal, vertical, right_inverse, below_inverse, right, below, below0,
-        southeast, schur, links,
+    below_inverse = passed(right_inverse, -1, 1)
+    schur, southeast, links = local_call(
+        diag_blocks, horizontal, vertical, e0, e1, scale0, scale1, y2, y3
     )
-    schur, links = last_call(from_left, from_above, schur, southwest, links)
+    schur0, links = right_call(horizontal, right_inverse, right, southeast, schur, links)
+    schur, schur1 = sides_call(from_left, from_above, schur0, schur)
+    schur, links = below_call(vertical, below_inverse, below, below0, southeast, from_left, schur1, schur, links)
     return (factor, schur, links)
 
 

time: 77.6 us -> 81.3 us (1.048)
  the two profiles are of different devices: /device:TPU:0 before, /device:TPU:96 now
where the time goes in v2:
time: 81.3 us; the launch traced here: 81.2 us
  Pallas kernels  37.6 us (46%)
  waiting for transfers between devices  29.2 us (36%)
  starting transfers between devices  9.73 us (12%)
  local copies, waits for them, and re-layouts  3.66 us (5%)
  between operations  0.89 us (1%)
    ppermute x7, waiting for transfers between devices, passed(): return lax.ppermute(value, ('row', 'col'), pairs)  29.2 us
    pallas_call x1, Pallas kernels, on_device(): state = factor_part(0, 2)(diag_blocks)  13.8 us
    pallas_call x1, Pallas kernels, on_device(): factor, e0, e1, scale0, scale1, packed = factor_part(2, 4)(*state)  10.9 us
    ppermute x7, starting transfers between devices, passed(): return lax.ppermute(value, ('row', 'col'), pairs)  9.73 us
    pallas_call x1, Pallas kernels, local_call(): call(local_kernel, (shape((2, N, N), F32), shape((2, N, N), F32), shape((...  4.57 us
    pallas_call x1, Pallas kernels, below_call(): call(below_kernel, (shape((2, 1, N, N), F32), shape((2, 1, 4, N, N), BF16...  3.3 us
    pallas_call x1, Pallas kernels, right_call(): call(right_kernel, (shape((N, N), F32), shape((2, 1, 4, N, N), BF16)), [A...  2.4 us
    unnamed x8, local copies, waits for them, and re-layouts  2.2 us
  transfers between devices with their start and end apart: 7, of which 3 were waited for; matrix products, arithmetic and copies ran while one was open for 0% of the time, Pallas kernels for 42%

profile of v2, /device:TPU:96, one launch (start us, length us, event | category | flops | bytes accessed | tf_op | source)
XLA Modules:
  0.0 81.2 jit_solution(6628798274944905273)
XLA Ops:
  0.6 1.4 %slice_bitcast_fusion = (bf16[512,512]{1,0:T(8,128)(2,1)S(1)}, bf16[1,512,512]{2,1,0:T(8,128)(2,1)S(1)}) fusion(bf16[2,2,512,512]{3,2,1,0:T(8,128)(2,1)} %h_ref.5), kind=kLoop, calls=%fused_computation.1 | loop fusion | bytes 2097152 | tf_op jit(solution)/shard_map/squeeze | solution.py:512
  2.1 2.4 %collective-permute-start.4 = (bf16[512,512]{1,0:T(8,128)(2,1)S(1)}, bf16[512,512]{1,0:T(8,128)(2,1)S(1)}, u32[]{:S(2)}, u32[]{:S(2)}) collective-permute-start(bf16[512,512]{1,0:T(8,128)(2,1)S(1)} %get-tuple-element.55), channel_id=1, source_target_pairs={{0,113},{1,114},{2,115},{3,116},{4,117},{5,118},{6,119},{7,120},{8... | collective-permute-start | bytes 1572872 | tf_op jit(solution)/shard_map/ppermute | solution.py:506
  4.5 0.1 pad_maximum_fusion
  4.6 2.4 %collective-permute-start.2 = (bf16[2,512,512]{2,1,0:T(8,128)(2,1)S(1)}, bf16[2,512,512]{2,1,0:T(8,128)(2,1)S(1)}, u32[]{:S(2)}, u32[]{:S(2)}) collective-permute-start(bf16[2,512,512]{2,1,0:T(8,128)(2,1)S(1)} %pad_maximum_fusion), channel_id=1, source_target_pairs={{0,15},{1,0},{2,1},{3,2},{4,3},{5,4},{6,5},{7,6},{8,7},{9,8},{10,9... | collective-permute-start | bytes 3145736 | tf_op jit(solution)/shard_map/ppermute | solution.py:506
  7.0 2.2 %copy-done.2 = f32[2,2,512,512]{3,2,1,0:T(8,128)S(1)} copy-done((f32[2,2,512,512]{3,2,1,0:T(8,128)S(1)}, f32[2,2,512,512]{3,2,1,0:T(8,128)}, u32[]{:S(2)}) %copy-start.2) | copy-done | bytes 4194328
  9.2 13.8 %shard_map.58 = (f32[2,1,512,512]{3,2,1,0:T(8,128)}, f32[256,512]{1,0:T(8,128)S(1)}, f32[256,512]{1,0:T(8,128)S(1)}, bf16[256,512]{1,0:T(8,128)(2,1)S(1)}, bf16[...) custom-call(f32[2,2,512,512]{3,2,1,0:T(8,128)S(1)} %copy-done.2), custom_call_target="tpu_custom_call" | custom-call | flops 30000001024 | bytes 4194304 | tf_op jit(solution)/shard_map/pallas_call | solution.py:513
  23.0 0.0 copy-start
  23.0 10.9 %shard_map.59 = (f32[2,1,512,512]{3,2,1,0:T(8,128)}, bf16[512,512]{1,0:T(8,128)(2,1)S(1)}, bf16[512,512]{1,0:T(8,128)(2,1)S(1)}, f32[512,128]{1,0:T(8,128)S(1)},...) custom-call(f32[2,1,512,512]{3,2,1,0:T(8,128)} %get-tuple-element.29.refs_0_, ...), custom_call_target="tpu_custom_call", output_to_operand_aliasing={{0}: (0, {})} | custom-call | flops 30000001024 | bytes 4194304 | tf_op jit(solution)/shard_map/pallas_call | solution.py:515
  33.8 0.9 %collective-permute-start = (bf16[1040,128]{1,0:T(8,128)(2,1)S(1)}, bf16[1040,128]{1,0:T(8,128)(2,1)S(1)}, u32[]{:S(2)}, u32[]{:S(2)}) collective-permute-start(bf16[1040,128]{1,0:T(8,128)(2,1)S(1)} %get-tuple-element.37), channel_id=1, source_target_pairs={{0,15},{1,0},{2,1},{3,2},{4,3},{5,4},{6,5},{7,6},{8,7},{9,8},{10,9... | collective-permute-start | bytes 798728 | tf_op jit(solution)/shard_map/ppermute | solution.py:506
  34.7 1.5 %shard_map.60 = (bf16[3088,128]{1,0:T(8,128)(2,1)S(1)}, bf16[1040,128]{1,0:T(8,128)(2,1)S(1)}, bf16[512,512]{1,0:T(8,128)(2,1)S(1)}, bf16[512,512]{1,0:T(8,128)(2,1)S(1)}) custom-call(bf16[2,2,512,512]{3,2,1,0:T(8,128)(2,1)S(1)} %copy-done, bf16[2,2,512,512]{3,2,1,0:T(8,128)(2,1)S(1)} %copy-done.1, bf16[512,512]{1,0:T(8,128)(2,1)S(1)} %get-tuple-element.39.e1, ...), custom_call_target="tpu_custom_call" | custom-call | flops 4000000000 | bytes 4194304 | tf_op jit(solution)/shard_map/pallas_call | solution.py:351
  36.3 2.4 %collective-permute-start.6 = (bf16[1040,128]{1,0:T(8,128)(2,1)S(1)}, bf16[1040,128]{1,0:T(8,128)(2,1)S(1)}, u32[]{:S(2)}, u32[]{:S(2)}) collective-permute-start(bf16[1040,128]{1,0:T(8,128)(2,1)S(1)} %get-tuple-element.46), channel_id=1, source_target_pairs={{0,16},{1,17},{2,18},{3,19},{4,20},{5,21},{6,22},{7,23},{8,24},{9,... | collective-permute-start | bytes 798728 | tf_op jit(solution)/shard_map/ppermute | solution.py:506
  38.7 0.0 collective-permute-start.5
  38.7 1.6 %collective-permute-start.3 = (bf16[2,512,512]{2,1,0:T(8,128)(2,1)S(1)}, bf16[2,512,512]{2,1,0:T(8,128)(2,1)S(1)}, u32[]{:S(2)}, u32[]{:S(2)}) collective-permute-start(bf16[2,512,512]{2,1,0:T(8,128)(2,1)S(1)} %collective-permute-done.2.rc), channel_id=1, source_target_pairs={{0,113},{1,114},{2,115},{3,116},{4,117},{5,118},{6,119},{7,120},{8... | collective-permute-start | bytes 3145736 | tf_op jit(solution)/shard_map/ppermute | solution.py:506
  40.2 4.6 %shard_map.61 = (f32[2,512,512]{2,1,0:T(8,128)S(1)}, f32[2,512,512]{2,1,0:T(8,128)S(1)}, bf16[2,1,4,512,512]{4,3,2,1,0:T(8,128)(2,1)}) custom-call(f32[2,2,512,512]{3,2,1,0:T(8,128)S(1)} %copy-done.3, bf16[2,2,512,512]{3,2,1,0:T(8,128)(2,1)S(1)} %copy-done, bf16[2,2,512,512]{3,2,1,0:T(8,128)(2,1)S(1)} %copy-done.1, ...), custom_call_target="tpu_custom_call" | custom-call | flops 8999999488 | bytes 4194304 | tf_op jit(solution)/shard_map/pallas_call | solution.py:399
  44.8 0.0 collective-permute-done.rpack
  44.8 0.1 collective-permute-start.1
  44.9 2.4 %shard_map.62 = (f32[512,512]{1,0:T(8,128)S(1)}, bf16[2,1,4,512,512]{4,3,2,1,0:T(8,128)(2,1)}) custom-call(bf16[2,2,512,512]{3,2,1,0:T(8,128)(2,1)S(1)} %copy-done, bf16[1040,128]{1,0:T(8,128)(2,1)S(1)} %collective-permute-done.rpack, bf16[2,512,512]{2,1,0:T(8,128)(2,1)S(1)} %collective-permute-done.2.rc, ...), custom_call_target="tpu_custom_call", output_to_operand_aliasing={{1}: (5, {})} | custom-call | flops 5000000000 | bytes 4194304 | tf_op jit(solution)/shard_map/pallas_call | solution.py:435
  47.3 0.9 %collective-permute-done.6.from_above = bf16[1040,128]{1,0:T(8,128)(2,1)S(1)} collective-permute-done((bf16[1040,128]{1,0:T(8,128)(2,1)S(1)}, bf16[1040,128]{1,0:T(8,128)(2,1)S(1)}, u32[]{:S(2)}, u32[]{:S(2)}) %collective-permute-start.6) | collective-permute-done | bytes 266272 | tf_op jit(solution)/shard_map/ppermute | solution.py:506
  48.2 13.7 %collective-permute-done.5.from_left = bf16[3088,128]{1,0:T(8,128)(2,1)S(1)} collective-permute-done((bf16[3088,128]{1,0:T(8,128)(2,1)S(1)}, bf16[3088,128]{1,0:T(8,128)(2,1)S(1)}, u32[]{:S(2)}, u32[]{:S(2)}) %collective-permute-start.5) | collective-permute-done | bytes 790560 | tf_op jit(solution)/shard_map/ppermute | solution.py:506
  62.0 1.2 %shard_map.63 = (f32[2,1,512,512]{3,2,1,0:T(8,128)}, f32[512,512]{1,0:T(8,128)S(1)}) custom-call(bf16[3088,128]{1,0:T(8,128)(2,1)S(1)} %collective-permute-done.5.from_left, bf16[1040,128]{1,0:T(8,128)(2,1)S(1)} %collective-permute-done.6.from_above, f32[512,512]{1,0:T(8,128)S(1)} %get-tuple-element.49.schur0, f32[2,512,512]{2,1,0:T(8,128)S(1)} %get-tuple-element.47.schur_in), custom_call_target="tpu_custom_call" | custom-call | flops 1000000000 | bytes 4194304 | tf_op jit(solution)/shard_map/pallas_call | solution.py:455
  63.1 0.0 collective-permute-done.4.bc0
  63.1 14.6 %collective-permute-done.1.bpack = bf16[1040,128]{1,0:T(8,128)(2,1)S(1)} collective-permute-done((bf16[1040,128]{1,0:T(8,128)(2,1)S(1)}, bf16[1040,128]{1,0:T(8,128)(2,1)S(1)}, u32[]{:S(2)}, u32[]{:S(2)}) %collective-permute-start.1) | collective-permute-done | bytes 266272 | tf_op jit(solution)/shard_map/ppermute | solution.py:506
  77.7 0.0 collective-permute-done.3.bc
  77.7 3.3 %shard_map.64 = (f32[2,1,512,512]{3,2,1,0:T(8,128)}, bf16[2,1,4,512,512]{4,3,2,1,0:T(8,128)(2,1)}) custom-call(bf16[2,2,512,512]{3,2,1,0:T(8,128)(2,1)S(1)} %copy-done.1, bf16[1040,128]{1,0:T(8,128)(2,1)S(1)} %collective-permute-done.1.bpack, bf16[2,512,512]{2,1,0:T(8,128)(2,1)S(1)} %collective-permute-done.3.bc, ...), custom_call_target="tpu_custom_call", output_to_operand_aliasing={{0}: (7, {}), {1}: (8, {})} | custom-call | flops 6000000000 | bytes 4194304 | tf_op jit(solution)/shard_map/pallas_call | solution.py:490
  (8 shorter events, 0.0 us)
Async XLA Ops:
  0.6 3.8 %copy-start.1 = (bf16[2,2,512,512]{3,2,1,0:T(8,128)(2,1)S(1)}, bf16[2,2,512,512]{3,2,1,0:T(8,128)(2,1)}, u32[]{:S(2)}) copy-start(bf16[2,2,512,512]{3,2,1,0:T(8,128)(2,1)} %v_ref.5) | copy-start | bytes 6291460
  2.1 61.1 %collective-permute-start.4 = (bf16[512,512]{1,0:T(8,128)(2,1)S(1)}, bf16[512,512]{1,0:T(8,128)(2,1)S(1)}, u32[]{:S(2)}, u32[]{:S(2)}) collective-permute-start(bf16[512,512]{1,0:T(8,128)(2,1)S(1)} %get-tuple-element.55), channel_id=1, source_target_pairs={{0,113},{1,114},{2,115},{3,116},{4,117},{5,118},{6,119},{7,120},{8... | collective-permute-start | bytes 1572872 | tf_op jit(solution)/shard_map/ppermute | solution.py:506
  4.6 34.1 %collective-permute-start.2 = (bf16[2,512,512]{2,1,0:T(8,128)(2,1)S(1)}, bf16[2,512,512]{2,1,0:T(8,128)(2,1)S(1)}, u32[]{:S(2)}, u32[]{:S(2)}) collective-permute-start(bf16[2,512,512]{2,1,0:T(8,128)(2,1)S(1)} %pad_maximum_fusion), channel_id=1, source_target_pairs={{0,15},{1,0},{2,1},{3,2},{4,3},{5,4},{6,5},{7,6},{8,7},{9,8},{10,9... | collective-permute-start | bytes 3145736 | tf_op jit(solution)/shard_map/ppermute | solution.py:506
  7.0 2.2 %copy-start.2 = (f32[2,2,512,512]{3,2,1,0:T(8,128)S(1)}, f32[2,2,512,512]{3,2,1,0:T(8,128)}, u32[]{:S(2)}) copy-start(f32[2,2,512,512]{3,2,1,0:T(8,128)} %d_ref.1) | copy-start | bytes 12582916
  23.0 11.8 %copy-start = (bf16[2,2,512,512]{3,2,1,0:T(8,128)(2,1)S(1)}, bf16[2,2,512,512]{3,2,1,0:T(8,128)(2,1)}, u32[]{:S(2)}) copy-start(bf16[2,2,512,512]{3,2,1,0:T(8,128)(2,1)} %h_ref.5) | copy-start | bytes 6291460
  33.8 11.0 %collective-permute-start = (bf16[1040,128]{1,0:T(8,128)(2,1)S(1)}, bf16[1040,128]{1,0:T(8,128)(2,1)S(1)}, u32[]{:S(2)}, u32[]{:S(2)}) collective-permute-start(bf16[1040,128]{1,0:T(8,128)(2,1)S(1)} %get-tuple-element.37), channel_id=1, source_target_pairs={{0,15},{1,0},{2,1},{3,2},{4,3},{5,4},{6,5},{7,6},{8,7},{9,8},{10,9... | collective-permute-start | bytes 798728 | tf_op jit(solution)/shard_map/ppermute | solution.py:506
  34.7 5.5 %copy-start.3 = (f32[2,2,512,512]{3,2,1,0:T(8,128)S(1)}, f32[2,2,512,512]{3,2,1,0:T(8,128)}, u32[]{:S(2)}) copy-start(f32[2,2,512,512]{3,2,1,0:T(8,128)} %d_ref.1) | copy-start | bytes 12582916
  36.3 12.0 %collective-permute-start.6 = (bf16[1040,128]{1,0:T(8,128)(2,1)S(1)}, bf16[1040,128]{1,0:T(8,128)(2,1)S(1)}, u32[]{:S(2)}, u32[]{:S(2)}) collective-permute-start(bf16[1040,128]{1,0:T(8,128)(2,1)S(1)} %get-tuple-element.46), channel_id=1, source_target_pairs={{0,16},{1,17},{2,18},{3,19},{4,20},{5,21},{6,22},{7,23},{8,24},{9,... | collective-permute-start | bytes 798728 | tf_op jit(solution)/shard_map/ppermute | solution.py:506
  38.7 23.3 %collective-permute-start.5 = (bf16[3088,128]{1,0:T(8,128)(2,1)S(1)}, bf16[3088,128]{1,0:T(8,128)(2,1)S(1)}, u32[]{:S(2)}, u32[]{:S(2)}) collective-permute-start(bf16[3088,128]{1,0:T(8,128)(2,1)S(1)} %get-tuple-element.45), channel_id=1, source_target_pairs={{0,1},{1,2},{2,3},{3,4},{4,5},{5,6},{6,7},{7,8},{8,9},{9,10},{10,1... | collective-permute-start | bytes 2371592 | tf_op jit(solution)/shard_map/ppermute | solution.py:506
  38.7 39.0 %collective-permute-start.3 = (bf16[2,512,512]{2,1,0:T(8,128)(2,1)S(1)}, bf16[2,512,512]{2,1,0:T(8,128)(2,1)S(1)}, u32[]{:S(2)}, u32[]{:S(2)}) collective-permute-start(bf16[2,512,512]{2,1,0:T(8,128)(2,1)S(1)} %collective-permute-done.2.rc), channel_id=1, source_target_pairs={{0,113},{1,114},{2,115},{3,116},{4,117},{5,118},{6,119},{7,120},{8... | collective-permute-start | bytes 3145736 | tf_op jit(solution)/shard_map/ppermute | solution.py:506
  44.8 32.9 %collective-permute-start.1 = (bf16[1040,128]{1,0:T(8,128)(2,1)S(1)}, bf16[1040,128]{1,0:T(8,128)(2,1)S(1)}, u32[]{:S(2)}, u32[]{:S(2)}) collective-permute-start(bf16[1040,128]{1,0:T(8,128)(2,1)S(1)} %collective-permute-done.rpack), channel_id=1, source_target_pairs={{0,113},{1,114},{2,115},{3,116},{4,117},{5,118},{6,119},{7,120},{8... | collective-permute-start | bytes 798728 | tf_op jit(solution)/shard_map/ppermute | solution.py:506

commit v3 on v2

--- a/solution.py
+++ b/solution.py
@@ -42,6 +42,7 @@
         for c in range(SB)
     ]
     pivots = [jnp.ones((8, NB), F32) for _ in range(2)]
+    inverses = [jnp.ones((8, NB), F32) for _ in range(2)]
     saved = [[xs[w][h] for h in range(2)] for w in range(2)]
     for k in range(SB):
         kh, kr = divmod(k, 8)
@@ -54,6 +55,7 @@
             head = rows8(cols[c][kh], kr)
             cols[c] = [cols[c][h] - mult[h] * head for h in range(2)]
         pivots[kh] = jnp.where(is_k, pivot, pivots[kh])
+        inverses[kh] = jnp.where(is_k, inverse, inverses[kh])
         for w in range(2):
             saved[w][kh] = jnp.where(is_k, xs[w][kh], saved[w][kh])
             head = rows8(xs[w][kh], kr)
@@ -67,7 +69,7 @@
     below = NB - k0 - SB
     if below:
         z = jnp.concatenate(
-            [jnp.concatenate([xs[w][h] / pivots[h] for w in range(2)], 1) for h in range(2)], 0
+            [jnp.concatenate([xs[w][h] * inverses[h] for w in range(2)], 1) for h in range(2)], 0
         )
         zh, zl = split(z)
 
@@ -91,7 +93,9 @@
     c_i = lax.broadcasted_iota(jnp.int32, (NB, NB), 1)
     wide = lax.broadcasted_iota(jnp.int32, (NB, N), 1)
     for l_ref in l_refs:
-        l_ref[...] = jnp.zeros_like(l_ref)
+        for c in range(first, last):
+            if c:
+                l_ref[0 : c * NB, c * NB : (c + 1) * NB] = jnp.zeros((c * NB, NB), F32)
 
     def outer(o, carry):
         base = pl.multiple_of(o * NB, NB)
@@ -441,34 +445,21 @@
     )(*args)
 
 
-def sides_kernel(from_left, from_above, schur0, schur_in, schur_out, schur1, sbuf, sem):
-    sbuf[...] = schur0[...]
-    add_symmetric(from_above, sbuf)
-    copy = pltpu.make_async_copy(sbuf, schur_out.at[0, 0], sem)
-    copy.start()
-    schur1[...] = schur_in[1]
-    add_symmetric(from_left, schur1)
-    copy.wait()
-
-
-def sides_call(*args):
-    return call(
-        sides_kernel, (shape((2, 1, N, N), F32), shape((N, N), F32)),
-        [VM] * 4, (ANY, VM), [WIDE, pltpu.SemaphoreType.DMA], 1, 6,
-    )(*args)
-
-
-def below_kernel(v_ref, bpack, bc, bc0, se, from_left, schur1, schur_in, link_in, schur_out, link_out,
+def below_kernel(v_ref, bpack, bc, bc0, se, from_left, from_above, schur0, schur_in, link_in, schur_out, link_out,
                  inv, c1, w0, w1, w2, w3, scale, row, lbuf, sbuf, in_sem, sem):
     load = pltpu.make_async_copy(v_ref.at[1, 0], c1, in_sem)
     load.start()
     unpack_unit(bpack, inv, scale, row)
+    sbuf[0] = schur0[...]
+    add_symmetric(from_above, sbuf.at[0])
+    stores = [pltpu.make_async_copy(sbuf.at[m], schur_out.at[m, 0], sem.at[3 + m]) for m in range(2)]
+    stores[0].start()
     load.wait()
     outs = []
     solve_t(inv, row, c1, w1)
-    sbuf[...] = schur1[...] - dot(w1[...], w1[...], 1, 1)
-    copy = pltpu.make_async_copy(sbuf, schur_out.at[1, 0], sem.at[3])
-    copy.start()
+    sbuf[1] = schur_in[1] - dot(w1[...], w1[...], 1, 1)
+    add_symmetric(from_left, sbuf.at[1])
+    stores[1].start()
     solve_n(inv, scale, bc.at[1], w3)
     put_link(outs, lbuf, link_out, sem, 1, 1, dot(w1[...], w3[...]))
     solve_n(inv, scale, bc.at[0], w2)
@@ -482,17 +473,17 @@
         0,
     )
     put_link(outs, lbuf, link_out, sem, 1, 3, dot(w1[...], w0[...], 1, 1) + side.astype(F32))
-    for c in outs + [copy]:
+    for c in outs + stores:
         c.wait()
 
 
 def below_call(*args):
     return call(
         below_kernel, (shape((2, 1, N, N), F32), shape((2, 1, 4, N, N), BF16)),
-        [ANY] + [VM] * 6 + [ANY, ANY], (ANY, ANY),
-        [B16] * 6 + [pltpu.VMEM((N, NB), F32), pltpu.VMEM((8, N), F32), pltpu.VMEM((3, N, N), BF16), WIDE]
-        + [pltpu.SemaphoreType.DMA, pltpu.SemaphoreType.DMA((4,))],
-        6, 12, {7: 0, 8: 1},
+        [ANY] + [VM] * 8 + [ANY], (ANY, ANY),
+        [B16] * 6 + [pltpu.VMEM((N, NB), F32), pltpu.VMEM((8, N), F32), pltpu.VMEM((3, N, N), BF16)]
+        + [pltpu.VMEM((2, N, N), F32), pltpu.SemaphoreType.DMA, pltpu.SemaphoreType.DMA((5,))],
+        6, 14, {9: 1},
     )(*args)
 
 
@@ -508,8 +499,9 @@
 
 def on_device(diag_blocks, horizontal, vertical):
     pair = jnp.stack([horizontal[0, 0], vertical[0, 0]])
+    own0, pair = lax.optimization_barrier((horizontal[0, 1], pair))
     right = passed(pair, 0, -1)
-    below0 = passed(horizontal[0, 1], -1, 1)
+    below0 = passed(own0, -1, 1)
     state = factor_part(0, 2)(diag_blocks)
     below = passed(right, -1, 1)
     factor, e0, e1, scale0, scale1, packed = factor_part(2, 4)(*state)
@@ -522,8 +514,9 @@
         diag_blocks, horizontal, vertical, e0, e1, scale0, scale1, y2, y3
     )
     schur0, links = right_call(horizontal, right_inverse, right, southeast, schur, links)
-    schur, schur1 = sides_call(from_left, from_above, schur0, schur)
-    schur, links = below_call(vertical, below_inverse, below, below0, southeast, from_left, schur1, schur, links)
+    schur, links = below_call(
+        vertical, below_inverse, below, below0, southeast, from_left, from_above, schur0, schur, links
+    )
     return (factor, schur, links)
 
 

time: 81.3 us -> 79.1 us (0.973)
  local copies, waits for them, and re-layouts: 3.66 us -> 1.63 us
  Pallas kernels: 37.6 us -> 36.3 us
  waiting for transfers between devices: 29.2 us -> 30.4 us
    unnamed x8 -> x6, local copies, waits for them, and re-layouts: 2.2 us -> 0.02 us
    another operation x1, local copies, waits for them, and re-layouts: 0.03 us -> 1.61 us  [on_device(): pair = jnp.stack([horizontal[0, 0], vertical[0, 0]])]
    squeeze x1 -> x0, local copies, waits for them, and re-layouts: 1.42 us -> none  [on_device(): below0 = passed(horizontal[0, 1], -1, 1)]
    ppermute x7, waiting for transfers between devices: 29.2 us -> 30.4 us  [passed(): return lax.ppermute(value, ('row', 'col'), pairs)]
    pallas_call x1 -> x0, Pallas kernels: 1.17 us -> none  [sides_call(): call(sides_kernel, (shape((2, 1, N, N), F32), shape((N, N), F32)), [VM] *...]
  transfers between devices with their start and end apart: 7 -> 7, of which waited for: 3 -> 2; matrix products, arithmetic and copies ran while one was open for 0% -> 0% of each run, Pallas kernels for 42% -> 42%
where the time goes in v3:
time: 79.1 us; the launch traced here: 79 us
  Pallas kernels  36.3 us (46%)
  waiting for transfers between devices  30.4 us (38%)
  starting transfers between devices  9.66 us (12%)
  local copies, waits for them, and re-layouts  1.63 us (2%)
  between operations  0.89 us (1%)
    ppermute x7, waiting for transfers between devices, passed(): return lax.ppermute(value, ('row', 'col'), pairs)  30.4 us
    pallas_call x1, Pallas kernels, on_device(): state = factor_part(0, 2)(diag_blocks)  13.6 us
    pallas_call x1, Pallas kernels, on_device(): factor, e0, e1, scale0, scale1, packed = factor_part(2, 4)(*state)  10.8 us
    ppermute x7, starting transfers between devices, passed(): return lax.ppermute(value, ('row', 'col'), pairs)  9.66 us
    pallas_call x1, Pallas kernels, local_call(): call(local_kernel, (shape((2, N, N), F32), shape((2, N, N), F32), shape((...  4.56 us
    pallas_call x1, Pallas kernels, below_call(): call(below_kernel, (shape((2, 1, N, N), F32), shape((2, 1, 4, N, N), BF16...  3.42 us
    pallas_call x1, Pallas kernels, right_call(): call(right_kernel, (shape((N, N), F32), shape((2, 1, 4, N, N), BF16)), [A...  2.39 us
    another operation x1, local copies, waits for them, and re-layouts, on_device(): pair = jnp.stack([horizontal[0, 0], vertical[0, 0]])  1.61 us
  transfers between devices with their start and end apart: 7, of which 2 were waited for; matrix products, arithmetic and copies ran while one was open for 0% of the time, Pallas kernels for 42%

profile of v3, /device:TPU:96, one launch (start us, length us, event | category | flops | bytes accessed | tf_op | source)
XLA Modules:
  0.0 79.0 jit_solution(5805775908647952997)
XLA Ops:
  0.6 1.6 %slice_bitcast_fusion.1 = (bf16[1,512,512]{2,1,0:T(8,128)(2,1)S(1)}, bf16[512,512]{1,0:T(8,128)(2,1)S(1)}, bf16[1,512,512]{2,1,0:T(8,128)(2,1)S(1)}) fusion(bf16[2,2,512,512]{3,2,1,0:T(8,128)(2,1)} %h_ref.5, bf16[2,2,512,512]{3,2,1,0:T(8,128)(2,1)} %v_ref.5), kind=kLoop, calls=%fused_computation.2 | loop fusion | bytes 3145728 | tf_op jit(solution)/shard_map/stack;squeeze | solution.py:501
  2.3 0.1 pad_maximum_fusion
  2.4 2.4 %collective-permute-start.4 = (bf16[512,512]{1,0:T(8,128)(2,1)S(1)}, bf16[512,512]{1,0:T(8,128)(2,1)S(1)}, u32[]{:S(2)}, u32[]{:S(2)}) collective-permute-start(bf16[512,512]{1,0:T(8,128)(2,1)S(1)} %get-tuple-element.39), channel_id=1, source_target_pairs={{0,113},{1,114},{2,115},{3,116},{4,117},{5,118},{6,119},{7,120},{8... | collective-permute-start | bytes 1572872 | tf_op jit(solution)/shard_map/ppermute | solution.py:497
  4.7 2.3 %collective-permute-start.2 = (bf16[2,512,512]{2,1,0:T(8,128)(2,1)S(1)}, bf16[2,512,512]{2,1,0:T(8,128)(2,1)S(1)}, u32[]{:S(2)}, u32[]{:S(2)}) collective-permute-start(bf16[2,512,512]{2,1,0:T(8,128)(2,1)S(1)} %pad_maximum_fusion), channel_id=1, source_target_pairs={{0,15},{1,0},{2,1},{3,2},{4,3},{5,4},{6,5},{7,6},{8,7},{9,8},{10,9... | collective-permute-start | bytes 3145736 | tf_op jit(solution)/shard_map/ppermute | solution.py:497
  7.1 13.6 %shard_map.58 = (f32[2,1,512,512]{3,2,1,0:T(8,128)}, f32[256,512]{1,0:T(8,128)S(1)}, f32[256,512]{1,0:T(8,128)S(1)}, bf16[256,512]{1,0:T(8,128)(2,1)S(1)}, bf16[...) custom-call(f32[2,2,512,512]{3,2,1,0:T(8,128)S(1)} %copy-done.2), custom_call_target="tpu_custom_call" | custom-call | flops 30000001024 | bytes 4194304 | tf_op jit(solution)/shard_map/pallas_call | solution.py:505
  20.7 0.0 copy-start
  20.7 0.0 copy-start.1
  20.8 10.8 %shard_map.59 = (f32[2,1,512,512]{3,2,1,0:T(8,128)}, bf16[512,512]{1,0:T(8,128)(2,1)S(1)}, bf16[512,512]{1,0:T(8,128)(2,1)S(1)}, f32[512,128]{1,0:T(8,128)S(1)},...) custom-call(f32[2,1,512,512]{3,2,1,0:T(8,128)} %get-tuple-element.29.refs_0_, ...), custom_call_target="tpu_custom_call", output_to_operand_aliasing={{0}: (0, {})} | custom-call | flops 30000001024 | bytes 4194304 | tf_op jit(solution)/shard_map/pallas_call | solution.py:507
  31.6 0.9 %collective-permute-start = (bf16[1040,128]{1,0:T(8,128)(2,1)S(1)}, bf16[1040,128]{1,0:T(8,128)(2,1)S(1)}, u32[]{:S(2)}, u32[]{:S(2)}) collective-permute-start(bf16[1040,128]{1,0:T(8,128)(2,1)S(1)} %get-tuple-element.37), channel_id=1, source_target_pairs={{0,15},{1,0},{2,1},{3,2},{4,3},{5,4},{6,5},{7,6},{8,7},{9,8},{10,9... | collective-permute-start | bytes 798728 | tf_op jit(solution)/shard_map/ppermute | solution.py:497
  32.5 1.5 %shard_map.60 = (bf16[3088,128]{1,0:T(8,128)(2,1)S(1)}, bf16[1040,128]{1,0:T(8,128)(2,1)S(1)}, bf16[512,512]{1,0:T(8,128)(2,1)S(1)}, bf16[512,512]{1,0:T(8,128)(2,1)S(1)}) custom-call(bf16[2,2,512,512]{3,2,1,0:T(8,128)(2,1)S(1)} %copy-done, bf16[2,2,512,512]{3,2,1,0:T(8,128)(2,1)S(1)} %copy-done.1, bf16[512,512]{1,0:T(8,128)(2,1)S(1)} %get-tuple-element.41.e1, ...), custom_call_target="tpu_custom_call" | custom-call | flops 4000000000 | bytes 4194304 | tf_op jit(solution)/shard_map/pallas_call | solution.py:355
  34.0 2.4 %collective-permute-start.6 = (bf16[1040,128]{1,0:T(8,128)(2,1)S(1)}, bf16[1040,128]{1,0:T(8,128)(2,1)S(1)}, u32[]{:S(2)}, u32[]{:S(2)}) collective-permute-start(bf16[1040,128]{1,0:T(8,128)(2,1)S(1)} %get-tuple-element.48), channel_id=1, source_target_pairs={{0,16},{1,17},{2,18},{3,19},{4,20},{5,21},{6,22},{7,23},{8,24},{9,... | collective-permute-start | bytes 798728 | tf_op jit(solution)/shard_map/ppermute | solution.py:497
  36.4 0.0 collective-permute-start.5
  36.4 0.0 collective-permute-done.2.rc
  36.4 1.6 %collective-permute-start.3 = (bf16[2,512,512]{2,1,0:T(8,128)(2,1)S(1)}, bf16[2,512,512]{2,1,0:T(8,128)(2,1)S(1)}, u32[]{:S(2)}, u32[]{:S(2)}) collective-permute-start(bf16[2,512,512]{2,1,0:T(8,128)(2,1)S(1)} %collective-permute-done.2.rc), channel_id=1, source_target_pairs={{0,113},{1,114},{2,115},{3,116},{4,117},{5,118},{6,119},{7,120},{8... | collective-permute-start | bytes 3145736 | tf_op jit(solution)/shard_map/ppermute | solution.py:497
  38.0 4.6 %shard_map.61 = (f32[2,512,512]{2,1,0:T(8,128)S(1)}, f32[2,512,512]{2,1,0:T(8,128)S(1)}, bf16[2,1,4,512,512]{4,3,2,1,0:T(8,128)(2,1)}) custom-call(f32[2,2,512,512]{3,2,1,0:T(8,128)S(1)} %copy-done.2, bf16[2,2,512,512]{3,2,1,0:T(8,128)(2,1)S(1)} %copy-done, bf16[2,2,512,512]{3,2,1,0:T(8,128)(2,1)S(1)} %copy-done.1, ...), custom_call_target="tpu_custom_call" | custom-call | flops 8999999488 | bytes 4194304 | tf_op jit(solution)/shard_map/pallas_call | solution.py:403
  42.5 0.0 collective-permute-done.rpack
  42.5 0.1 collective-permute-start.1
  42.6 2.4 %shard_map.62 = (f32[512,512]{1,0:T(8,128)S(1)}, bf16[2,1,4,512,512]{4,3,2,1,0:T(8,128)(2,1)}) custom-call(bf16[2,2,512,512]{3,2,1,0:T(8,128)(2,1)S(1)} %copy-done, bf16[1040,128]{1,0:T(8,128)(2,1)S(1)} %collective-permute-done.rpack, bf16[2,512,512]{2,1,0:T(8,128)(2,1)S(1)} %collective-permute-done.2.rc, ...), custom_call_target="tpu_custom_call", output_to_operand_aliasing={{1}: (5, {})} | custom-call | flops 5000000000 | bytes 4194304 | tf_op jit(solution)/shard_map/pallas_call | solution.py:439
  45.0 0.9 %collective-permute-done.6.from_above = bf16[1040,128]{1,0:T(8,128)(2,1)S(1)} collective-permute-done((bf16[1040,128]{1,0:T(8,128)(2,1)S(1)}, bf16[1040,128]{1,0:T(8,128)(2,1)S(1)}, u32[]{:S(2)}, u32[]{:S(2)}) %collective-permute-start.6) | collective-permute-done | bytes 266272 | tf_op jit(solution)/shard_map/ppermute | solution.py:497
  45.9 0.0 collective-permute-done.4.bc0
  45.9 29.5 %collective-permute-done.1.bpack = bf16[1040,128]{1,0:T(8,128)(2,1)S(1)} collective-permute-done((bf16[1040,128]{1,0:T(8,128)(2,1)S(1)}, bf16[1040,128]{1,0:T(8,128)(2,1)S(1)}, u32[]{:S(2)}, u32[]{:S(2)}) %collective-permute-start.1) | collective-permute-done | bytes 266272 | tf_op jit(solution)/shard_map/ppermute | solution.py:497
  75.4 0.0 collective-permute-done.5.from_left
  75.4 0.0 collective-permute-done.3.bc
  75.4 3.4 %shard_map.63 = (f32[2,1,512,512]{3,2,1,0:T(8,128)}, bf16[2,1,4,512,512]{4,3,2,1,0:T(8,128)(2,1)}) custom-call(bf16[2,2,512,512]{3,2,1,0:T(8,128)(2,1)S(1)} %copy-done.1, bf16[1040,128]{1,0:T(8,128)(2,1)S(1)} %collective-permute-done.1.bpack, bf16[2,512,512]{2,1,0:T(8,128)(2,1)S(1)} %collective-permute-done.3.bc, ...), custom_call_target="tpu_custom_call", output_to_operand_aliasing={{1}: (9, {})} | custom-call | flops 6000000000 | bytes 4194304 | tf_op jit(solution)/shard_map/pallas_call | solution.py:481
  (4 shorter events, 0.0 us)
Async XLA Ops:
  0.6 6.5 %copy-start.2 = (f32[2,2,512,512]{3,2,1,0:T(8,128)S(1)}, f32[2,2,512,512]{3,2,1,0:T(8,128)}, u32[]{:S(2)}) copy-start(f32[2,2,512,512]{3,2,1,0:T(8,128)} %d_ref.1) | copy-start | bytes 12582916
  2.4 43.6 %collective-permute-start.4 = (bf16[512,512]{1,0:T(8,128)(2,1)S(1)}, bf16[512,512]{1,0:T(8,128)(2,1)S(1)}, u32[]{:S(2)}, u32[]{:S(2)}) collective-permute-start(bf16[512,512]{1,0:T(8,128)(2,1)S(1)} %get-tuple-element.39), channel_id=1, source_target_pairs={{0,113},{1,114},{2,115},{3,116},{4,117},{5,118},{6,119},{7,120},{8... | collective-permute-start | bytes 1572872 | tf_op jit(solution)/shard_map/ppermute | solution.py:497
  4.7 31.7 %collective-permute-start.2 = (bf16[2,512,512]{2,1,0:T(8,128)(2,1)S(1)}, bf16[2,512,512]{2,1,0:T(8,128)(2,1)S(1)}, u32[]{:S(2)}, u32[]{:S(2)}) collective-permute-start(bf16[2,512,512]{2,1,0:T(8,128)(2,1)S(1)} %pad_maximum_fusion), channel_id=1, source_target_pairs={{0,15},{1,0},{2,1},{3,2},{4,3},{5,4},{6,5},{7,6},{8,7},{9,8},{10,9... | collective-permute-start | bytes 3145736 | tf_op jit(solution)/shard_map/ppermute | solution.py:497
  20.7 11.7 %copy-start = (bf16[2,2,512,512]{3,2,1,0:T(8,128)(2,1)S(1)}, bf16[2,2,512,512]{3,2,1,0:T(8,128)(2,1)}, u32[]{:S(2)}) copy-start(bf16[2,2,512,512]{3,2,1,0:T(8,128)(2,1)} %h_ref.5) | copy-start | bytes 6291460
  20.7 11.7 %copy-start.1 = (bf16[2,2,512,512]{3,2,1,0:T(8,128)(2,1)S(1)}, bf16[2,2,512,512]{3,2,1,0:T(8,128)(2,1)}, u32[]{:S(2)}) copy-start(bf16[2,2,512,512]{3,2,1,0:T(8,128)(2,1)} %v_ref.5) | copy-start | bytes 6291460
  31.6 10.9 %collective-permute-start = (bf16[1040,128]{1,0:T(8,128)(2,1)S(1)}, bf16[1040,128]{1,0:T(8,128)(2,1)S(1)}, u32[]{:S(2)}, u32[]{:S(2)}) collective-permute-start(bf16[1040,128]{1,0:T(8,128)(2,1)S(1)} %get-tuple-element.37), channel_id=1, source_target_pairs={{0,15},{1,0},{2,1},{3,2},{4,3},{5,4},{6,5},{7,6},{8,7},{9,8},{10,9... | collective-permute-start | bytes 798728 | tf_op jit(solution)/shard_map/ppermute | solution.py:497
  34.0 12.0 %collective-permute-start.6 = (bf16[1040,128]{1,0:T(8,128)(2,1)S(1)}, bf16[1040,128]{1,0:T(8,128)(2,1)S(1)}, u32[]{:S(2)}, u32[]{:S(2)}) collective-permute-start(bf16[1040,128]{1,0:T(8,128)(2,1)S(1)} %get-tuple-element.48), channel_id=1, source_target_pairs={{0,16},{1,17},{2,18},{3,19},{4,20},{5,21},{6,22},{7,23},{8,24},{9,... | collective-permute-start | bytes 798728 | tf_op jit(solution)/shard_map/ppermute | solution.py:497
  36.4 39.0 %collective-permute-start.5 = (bf16[3088,128]{1,0:T(8,128)(2,1)S(1)}, bf16[3088,128]{1,0:T(8,128)(2,1)S(1)}, u32[]{:S(2)}, u32[]{:S(2)}) collective-permute-start(bf16[3088,128]{1,0:T(8,128)(2,1)S(1)} %get-tuple-element.47), channel_id=1, source_target_pairs={{0,1},{1,2},{2,3},{3,4},{4,5},{5,6},{6,7},{7,8},{8,9},{9,10},{10,1... | collective-permute-start | bytes 2371592 | tf_op jit(solution)/shard_map/ppermute | solution.py:497
  36.4 39.0 %collective-permute-start.3 = (bf16[2,512,512]{2,1,0:T(8,128)(2,1)S(1)}, bf16[2,512,512]{2,1,0:T(8,128)(2,1)S(1)}, u32[]{:S(2)}, u32[]{:S(2)}) collective-permute-start(bf16[2,512,512]{2,1,0:T(8,128)(2,1)S(1)} %collective-permute-done.2.rc), channel_id=1, source_target_pairs={{0,113},{1,114},{2,115},{3,116},{4,117},{5,118},{6,119},{7,120},{8... | collective-permute-start | bytes 3145736 | tf_op jit(solution)/shard_map/ppermute | solution.py:497
  42.5 32.9 %collective-permute-start.1 = (bf16[1040,128]{1,0:T(8,128)(2,1)S(1)}, bf16[1040,128]{1,0:T(8,128)(2,1)S(1)}, u32[]{:S(2)}, u32[]{:S(2)}) collective-permute-start(bf16[1040,128]{1,0:T(8,128)(2,1)S(1)} %collective-permute-done.rpack), channel_id=1, source_target_pairs={{0,113},{1,114},{2,115},{3,116},{4,117},{5,118},{6,119},{7,120},{8... | collective-permute-start | bytes 798728 | tf_op jit(solution)/shard_map/ppermute | solution.py:497

commit v4 on v3

--- a/solution.py
+++ b/solution.py
@@ -95,11 +95,12 @@
     for l_ref in l_refs:
         for c in range(first, last):
             if c:
-                l_ref[0 : c * NB, c * NB : (c + 1) * NB] = jnp.zeros((c * NB, NB), F32)
+                l_ref[0 : c * NB, (c - first) * NB : (c - first + 1) * NB] = jnp.zeros((c * NB, NB), F32)
 
     def outer(o, carry):
         base = pl.multiple_of(o * NB, NB)
         here = pl.ds(base, NB)
+        there = pl.ds(pl.multiple_of(base - first * NB, NB), NB)
         for g_ref, x_ref in zip(g_refs, x_refs):
             x_ref[:, 0:NB] = g_ref[here, here]
             x_ref[:, NB : 2 * NB] = jnp.where(r_i == c_i, 1.0, 0.0)
@@ -108,7 +109,7 @@
                 eliminate(s, x_ref, p_ref, s_ref)
         for m in range(2):
             p_ref, s_ref, w_ref = p_refs[m], s_refs[m], w_refs[m]
-            l_refs[m][here, here] = jnp.where(r_i >= c_i, p_ref[:, 0:NB].T, 0.0)
+            l_refs[m][here, there] = jnp.where(r_i >= c_i, p_ref[:, 0:NB].T, 0.0)
             inverse = p_ref[:, NB : 2 * NB]
             w_ref[...] = dot3(split(inverse), split(g_refs[m][here, :]))
             w_ref[:, here] = inverse
@@ -122,7 +123,7 @@
             def _():
                 for g_ref, p_ref, w_ref, l_ref in zip(g_refs, p_refs, w_refs, l_refs):
                     lower = dot3(split(g_ref[rows, here]), split(p_ref[:, NB : 2 * NB]), 1)
-                    l_ref[rows, here] = lower
+                    l_ref[rows, there] = lower
                     g_ref[rows, here] = jnp.zeros((NB, NB), F32)
                     g_ref[rows, :] = g_ref[rows, :] - dot3(split(lower), split(w_ref[...]))
 
@@ -268,7 +269,7 @@
     )
 
 
-WORK = [pltpu.VMEM((NB, 2 * NB), F32)] * 6 + [pltpu.VMEM((NB, N), F32)] * 2 + [WIDE] * 4
+WORK = [pltpu.VMEM((NB, 2 * NB), F32)] * 6 + [pltpu.VMEM((NB, N), F32)] * 2 + [WIDE] * 2
 DMA2 = pltpu.SemaphoreType.DMA((2,))
 ENDS = (shape((N, N), BF16), shape((N, N), BF16), shape((N, NB), F32), shape((N, NB), F32))
 
@@ -280,13 +281,13 @@
     def kernel(*refs):
         refs = list(refs)
         take = lambda n: [refs.pop(0) for _ in range(n)]
-        source = take(1)[0]
+        source = None if first else take(1)[0]
         before = take(6) if first else ()
-        l_out = take(1)[0]
+        l0, l1 = take(2)
         after = take(5) if ending else take(6)
-        x0, x1, p0, p1, s0, s1, w0, w1, g0, g1, l0, l1 = take(12)
+        x0, x1, p0, p1, s0, s1, w0, w1, g0, g1 = take(10)
         state = tuple(after[:4]) if ending else tuple(take(4))
-        in_sem, out_sem = take(2)
+        in_sem = take(1)[0]
         if first:
             for dst, src in zip((g0, g1), before):
                 dst[lo:N, :] = src[...]
@@ -302,12 +303,6 @@
             for c in copies:
                 c.wait()
         factor_steps(first, last, (g0, g1), (x0, x1), (p0, p1), (s0, s1), (w0, w1), (l0, l1), state[:2], state[2:])
-        outs = [
-            pltpu.make_async_copy(l_ref.at[:, lo:hi], l_out.at[m, 0, :, lo:hi], out_sem.at[m])
-            for m, l_ref in enumerate((l0, l1))
-        ]
-        for c in outs:
-            c.start()
         if ending:
             pack_unit(state[0], state[2], after[4])
         else:
@@ -315,8 +310,6 @@
                 dst[...] = src[hi:N, :]
             for dst, src in zip(after[2:], state):
                 dst[...] = src[0:hi, :]
-        for c in outs:
-            c.wait()
 
     if ending:
         outs = ENDS + (shape((PACKED, NB), BF16),)
@@ -325,9 +318,9 @@
         outs = (shape((N - hi, N), F32),) * 2 + (shape((hi, N), BF16),) * 2 + (shape((hi, NB), F32),) * 2
         scratch = [B16, B16, pltpu.VMEM((N, NB), F32), pltpu.VMEM((N, NB), F32)]
     return call(
-        kernel, (shape((2, 1, N, N), F32),) + outs,
-        [ANY] + [VM] * (6 if first else 0), (ANY,) + (VM,) * len(outs),
-        WORK + scratch + [DMA2, DMA2], 15 * (last - first), 13, {0: 0} if first else None,
+        kernel, (shape((N, hi - lo), F32),) * 2 + outs,
+        [VM] * 6 if first else [ANY], (VM,) * (2 + len(outs)),
+        WORK + scratch + [DMA2], 15 * (last - first), 13,
     )
 
 
@@ -360,8 +353,9 @@
     )(*args)
 
 
-def local_kernel(d_ref, h_ref, v_ref, e0, e1, scale0, scale1, y2, y3, sbuf, dbuf, link_out,
-                 c0, c1, f2, f3, y0, y1, z2, z3, lbuf, row1, in_sem, out_sem):
+def local_kernel(d_ref, h_ref, v_ref, e0, e1, scale0, scale1, y2, y3, la0, la1, lb0, lb1,
+                 l_out, sbuf, dbuf, link_out,
+                 c0, c1, f2, f3, y0, y1, z2, z3, lbuf, row1, in_sem, out_sem, l_sem):
     copies = [
         pltpu.make_async_copy(src, dst, in_sem.at[k])
         for k, (src, dst) in enumerate(
@@ -376,6 +370,13 @@
         )
     ]
     for c in copies:
+        c.start()
+    half = N // 2
+    factors = [
+        pltpu.make_async_copy(src, l_out.at[k % 2, 0, :, k // 2 * half : (k // 2 + 1) * half], l_sem.at[k])
+        for k, src in enumerate((la0, la1, lb0, lb1))
+    ]
+    for c in factors:
         c.start()
     scale_row(scale1, row1)
     for c in copies[:4]:
@@ -395,17 +396,17 @@
         c.wait()
     sbuf[0] = sbuf[0] - (dot(u2, z2[...]) + dot(y1[...], y1[...], 1, 1))
     sbuf[1] = sbuf[1] - (dot(z3[...].T, z3[...]) + dot(y0[...], y0[...], 1, 1))
-    for c in outs:
+    for c in outs + factors:
         c.wait()
 
 
 def local_call(*args):
     return call(
         local_kernel,
-        (shape((2, N, N), F32), shape((2, N, N), F32), shape((2, 1, 4, N, N), BF16)),
-        [ANY] * 3 + [VM] * 6, (VM, VM, ANY),
+        (shape((2, 1, N, N), F32), shape((2, N, N), F32), shape((2, N, N), F32), shape((2, 1, 4, N, N), BF16)),
+        [ANY] * 3 + [VM] * 10, (ANY, VM, VM, ANY),
         [B16] * 8 + [pltpu.VMEM((3, N, N), BF16), pltpu.VMEM((8, N), F32)]
-        + [pltpu.SemaphoreType.DMA((6,)), pltpu.SemaphoreType.DMA((3,))],
+        + [pltpu.SemaphoreType.DMA((6,)), pltpu.SemaphoreType.DMA((3,)), pltpu.SemaphoreType.DMA((4,))],
         9, 16,
     )(*args)
 
@@ -502,16 +503,16 @@
     own0, pair = lax.optimization_barrier((horizontal[0, 1], pair))
     right = passed(pair, 0, -1)
     below0 = passed(own0, -1, 1)
-    state = factor_part(0, 2)(diag_blocks)
+    la0, la1, *state = factor_part(0, 2)(diag_blocks)
     below = passed(right, -1, 1)
-    factor, e0, e1, scale0, scale1, packed = factor_part(2, 4)(*state)
+    lb0, lb1, e0, e1, scale0, scale1, packed = factor_part(2, 4)(*state)
     right_inverse = passed(packed, 0, -1)
     to_right, to_below, y2, y3 = products_call(horizontal, vertical, e1, scale1)
     from_left = passed(to_right, 0, 1)
     from_above = passed(to_below, 1, 0)
     below_inverse = passed(right_inverse, -1, 1)
-    schur, southeast, links = local_call(
-        diag_blocks, horizontal, vertical, e0, e1, scale0, scale1, y2, y3
+    factor, schur, southeast, links = local_call(
+        diag_blocks, horizontal, vertical, e0, e1, scale0, scale1, y2, y3, la0, la1, lb0, lb1
     )
     schur0, links = right_call(horizontal, right_inverse, right, southeast, schur, links)
     schur, links = below_call(

time: 79.1 us -> 77.4 us (0.979)
  Pallas kernels: 36.3 us -> 34.6 us
    pallas_call x3, Pallas kernels: 29 us -> 27.3 us  [the longest x1 12.8 us: on_device(): la0, la1, *state = factor_part(0, 2)(diag_blocks)]
  transfers between devices with their start and end apart: 7 -> 7, of which waited for: 2 -> 2; matrix products, arithmetic and copies ran while one was open for 0% -> 0% of each run, Pallas kernels for 42% -> 40%
where the time goes in v4:
time: 77.4 us; the launch traced here: 77.2 us
  Pallas kernels  34.6 us (45%)
  waiting for transfers between devices  30.4 us (39%)
  starting transfers between devices  9.67 us (12%)
  local copies, waits for them, and re-layouts  1.63 us (2%)
  between operations  0.89 us (1%)
    ppermute x7, waiting for transfers between devices, passed(): return lax.ppermute(value, ('row', 'col'), pairs)  30.4 us
    pallas_call x1, Pallas kernels, on_device(): la0, la1, *state = factor_part(0, 2)(diag_blocks)  12.8 us
    pallas_call x1, Pallas kernels, on_device(): lb0, lb1, e0, e1, scale0, scale1, packed = factor_part(2, 4)(*state)  9.92 us
    ppermute x7, starting transfers between devices, passed(): return lax.ppermute(value, ('row', 'col'), pairs)  9.67 us
    pallas_call x1, Pallas kernels, local_call(): call(local_kernel, (shape((2, 1, N, N), F32), shape((2, N, N), F32), shap...  4.59 us
    pallas_call x1, Pallas kernels, below_call(): call(below_kernel, (shape((2, 1, N, N), F32), shape((2, 1, 4, N, N), BF16...  3.42 us
    pallas_call x1, Pallas kernels, right_call(): call(right_kernel, (shape((N, N), F32), shape((2, 1, 4, N, N), BF16)), [A...  2.39 us
    another operation x1, local copies, waits for them, and re-layouts, on_device(): pair = jnp.stack([horizontal[0, 0], vertical[0, 0]])  1.61 us
  transfers between devices with their start and end apart: 7, of which 2 were waited for; matrix products, arithmetic and copies ran while one was open for 0% of the time, Pallas kernels for 40%

profile of v4, /device:TPU:96, one launch (start us, length us, event | category | flops | bytes accessed | tf_op | source)
XLA Modules:
  0.0 77.2 jit_solution(887176797489434748)
XLA Ops:
  0.6 1.6 %slice_bitcast_fusion.1 = (bf16[1,512,512]{2,1,0:T(8,128)(2,1)S(1)}, bf16[512,512]{1,0:T(8,128)(2,1)S(1)}, bf16[1,512,512]{2,1,0:T(8,128)(2,1)S(1)}) fusion(bf16[2,2,512,512]{3,2,1,0:T(8,128)(2,1)} %h_ref.5, bf16[2,2,512,512]{3,2,1,0:T(8,128)(2,1)} %v_ref.5), kind=kLoop, calls=%fused_computation.2 | loop fusion | bytes 3145728 | tf_op jit(solution)/shard_map/stack;squeeze | solution.py:502
  2.3 0.1 pad_maximum_fusion
  2.4 2.4 %collective-permute-start.4 = (bf16[512,512]{1,0:T(8,128)(2,1)S(1)}, bf16[512,512]{1,0:T(8,128)(2,1)S(1)}, u32[]{:S(2)}, u32[]{:S(2)}) collective-permute-start(bf16[512,512]{1,0:T(8,128)(2,1)S(1)} %get-tuple-element.51), channel_id=1, source_target_pairs={{0,113},{1,114},{2,115},{3,116},{4,117},{5,118},{6,119},{7,120},{8... | collective-permute-start | bytes 1572872 | tf_op jit(solution)/shard_map/ppermute | solution.py:498
  4.7 2.3 %collective-permute-start.2 = (bf16[2,512,512]{2,1,0:T(8,128)(2,1)S(1)}, bf16[2,512,512]{2,1,0:T(8,128)(2,1)S(1)}, u32[]{:S(2)}, u32[]{:S(2)}) collective-permute-start(bf16[2,512,512]{2,1,0:T(8,128)(2,1)S(1)} %pad_maximum_fusion), channel_id=1, source_target_pairs={{0,15},{1,0},{2,1},{3,2},{4,3},{5,4},{6,5},{7,6},{8,7},{9,8},{10,9... | collective-permute-start | bytes 3145736 | tf_op jit(solution)/shard_map/ppermute | solution.py:498
  7.1 12.8 %shard_map.58 = (f32[512,256]{1,0:T(8,128)S(1)}, f32[512,256]{1,0:T(8,128)S(1)}, f32[256,512]{1,0:T(8,128)S(1)}, f32[256,512]{1,0:T(8,128)S(1)}, bf16[256,512]{1...) custom-call(f32[2,2,512,512]{3,2,1,0:T(8,128)S(1)} %copy-done.2), custom_call_target="tpu_custom_call" | custom-call | flops 30000001024 | bytes 4194304 | tf_op jit(solution)/shard_map/pallas_call | solution.py:506
  19.9 0.0 copy-start
  19.9 0.0 copy-start.1
  19.9 9.9 %shard_map.59 = (f32[512,256]{1,0:T(8,128)S(1)}, f32[512,256]{1,0:T(8,128)S(1)}, bf16[512,512]{1,0:T(8,128)(2,1)S(1)}, bf16[512,512]{1,0:T(8,128)(2,1)S(1)}, f32...) custom-call(f32[256,512]{1,0:T(8,128)S(1)} %get-tuple-element.32.refs_0_, ...), custom_call_target="tpu_custom_call" | custom-call | flops 30000001024 | bytes 4194304 | tf_op jit(solution)/shard_map/pallas_call | solution.py:508
  29.8 0.9 %collective-permute-start = (bf16[1040,128]{1,0:T(8,128)(2,1)S(1)}, bf16[1040,128]{1,0:T(8,128)(2,1)S(1)}, u32[]{:S(2)}, u32[]{:S(2)}) collective-permute-start(bf16[1040,128]{1,0:T(8,128)(2,1)S(1)} %get-tuple-element.49), channel_id=1, source_target_pairs={{0,15},{1,0},{2,1},{3,2},{4,3},{5,4},{6,5},{7,6},{8,7},{9,8},{10,9... | collective-permute-start | bytes 798728 | tf_op jit(solution)/shard_map/ppermute | solution.py:498
  30.7 1.5 %shard_map.60 = (bf16[3088,128]{1,0:T(8,128)(2,1)S(1)}, bf16[1040,128]{1,0:T(8,128)(2,1)S(1)}, bf16[512,512]{1,0:T(8,128)(2,1)S(1)}, bf16[512,512]{1,0:T(8,128)(2,1)S(1)}) custom-call(bf16[2,2,512,512]{3,2,1,0:T(8,128)(2,1)S(1)} %copy-done, bf16[2,2,512,512]{3,2,1,0:T(8,128)(2,1)S(1)} %copy-done.1, bf16[512,512]{1,0:T(8,128)(2,1)S(1)} %get-tuple-element.39.e1, ...), custom_call_target="tpu_custom_call" | custom-call | flops 4000000000 | bytes 4194304 | tf_op jit(solution)/shard_map/pallas_call | solution.py:348
  32.2 2.4 %collective-permute-start.6 = (bf16[1040,128]{1,0:T(8,128)(2,1)S(1)}, bf16[1040,128]{1,0:T(8,128)(2,1)S(1)}, u32[]{:S(2)}, u32[]{:S(2)}) collective-permute-start(bf16[1040,128]{1,0:T(8,128)(2,1)S(1)} %get-tuple-element.54), channel_id=1, source_target_pairs={{0,16},{1,17},{2,18},{3,19},{4,20},{5,21},{6,22},{7,23},{8,24},{9,... | collective-permute-start | bytes 798728 | tf_op jit(solution)/shard_map/ppermute | solution.py:498
  34.6 0.0 collective-permute-start.5
  34.6 0.0 collective-permute-done.2.rc
  34.6 1.6 %collective-permute-start.3 = (bf16[2,512,512]{2,1,0:T(8,128)(2,1)S(1)}, bf16[2,512,512]{2,1,0:T(8,128)(2,1)S(1)}, u32[]{:S(2)}, u32[]{:S(2)}) collective-permute-start(bf16[2,512,512]{2,1,0:T(8,128)(2,1)S(1)} %collective-permute-done.2.rc), channel_id=1, source_target_pairs={{0,113},{1,114},{2,115},{3,116},{4,117},{5,118},{6,119},{7,120},{8... | collective-permute-start | bytes 3145736 | tf_op jit(solution)/shard_map/ppermute | solution.py:498
  36.2 4.6 %shard_map.61 = (f32[2,1,512,512]{3,2,1,0:T(8,128)}, f32[2,512,512]{2,1,0:T(8,128)S(1)}, f32[2,512,512]{2,1,0:T(8,128)S(1)}, bf16[2,1,4,512,512]{4,3,2,1,0:T(8,128)(2,1)}) custom-call(f32[2,2,512,512]{3,2,1,0:T(8,128)S(1)} %copy-done.2, bf16[2,2,512,512]{3,2,1,0:T(8,128)(2,1)S(1)} %copy-done, bf16[2,2,512,512]{3,2,1,0:T(8,128)(2,1)S(1)} %copy-done.1, ...), custom_call_target="tpu_custom_call" | custom-call | flops 8999999488 | bytes 4194304 | tf_op jit(solution)/shard_map/pallas_call | solution.py:404
  40.8 0.0 collective-permute-done.rpack
  40.8 0.1 collective-permute-start.1
  40.9 2.4 %shard_map.62 = (f32[512,512]{1,0:T(8,128)S(1)}, bf16[2,1,4,512,512]{4,3,2,1,0:T(8,128)(2,1)}) custom-call(bf16[2,2,512,512]{3,2,1,0:T(8,128)(2,1)S(1)} %copy-done, bf16[1040,128]{1,0:T(8,128)(2,1)S(1)} %collective-permute-done.rpack, bf16[2,512,512]{2,1,0:T(8,128)(2,1)S(1)} %collective-permute-done.2.rc, ...), custom_call_target="tpu_custom_call", output_to_operand_aliasing={{1}: (5, {})} | custom-call | flops 5000000000 | bytes 4194304 | tf_op jit(solution)/shard_map/pallas_call | solution.py:440
  43.3 0.9 %collective-permute-done.6.from_above = bf16[1040,128]{1,0:T(8,128)(2,1)S(1)} collective-permute-done((bf16[1040,128]{1,0:T(8,128)(2,1)S(1)}, bf16[1040,128]{1,0:T(8,128)(2,1)S(1)}, u32[]{:S(2)}, u32[]{:S(2)}) %collective-permute-start.6) | collective-permute-done | bytes 266272 | tf_op jit(solution)/shard_map/ppermute | solution.py:498
  44.2 0.0 collective-permute-done.4.bc0
  44.2 29.5 %collective-permute-done.1.bpack = bf16[1040,128]{1,0:T(8,128)(2,1)S(1)} collective-permute-done((bf16[1040,128]{1,0:T(8,128)(2,1)S(1)}, bf16[1040,128]{1,0:T(8,128)(2,1)S(1)}, u32[]{:S(2)}, u32[]{:S(2)}) %collective-permute-start.1) | collective-permute-done | bytes 266272 | tf_op jit(solution)/shard_map/ppermute | solution.py:498
  73.7 0.0 collective-permute-done.5.from_left
  73.7 0.0 collective-permute-done.3.bc
  73.7 3.4 %shard_map.63 = (f32[2,1,512,512]{3,2,1,0:T(8,128)}, bf16[2,1,4,512,512]{4,3,2,1,0:T(8,128)(2,1)}) custom-call(bf16[2,2,512,512]{3,2,1,0:T(8,128)(2,1)S(1)} %copy-done.1, bf16[1040,128]{1,0:T(8,128)(2,1)S(1)} %collective-permute-done.1.bpack, bf16[2,512,512]{2,1,0:T(8,128)(2,1)S(1)} %collective-permute-done.3.bc, ...), custom_call_target="tpu_custom_call", output_to_operand_aliasing={{1}: (9, {})} | custom-call | flops 6000000000 | bytes 4194304 | tf_op jit(solution)/shard_map/pallas_call | solution.py:482
  (4 shorter events, 0.0 us)
Async XLA Ops:
  0.6 6.5 %copy-start.2 = (f32[2,2,512,512]{3,2,1,0:T(8,128)S(1)}, f32[2,2,512,512]{3,2,1,0:T(8,128)}, u32[]{:S(2)}) copy-start(f32[2,2,512,512]{3,2,1,0:T(8,128)} %d_ref.1) | copy-start | bytes 12582916
  2.4 41.8 %collective-permute-start.4 = (bf16[512,512]{1,0:T(8,128)(2,1)S(1)}, bf16[512,512]{1,0:T(8,128)(2,1)S(1)}, u32[]{:S(2)}, u32[]{:S(2)}) collective-permute-start(bf16[512,512]{1,0:T(8,128)(2,1)S(1)} %get-tuple-element.51), channel_id=1, source_target_pairs={{0,113},{1,114},{2,115},{3,116},{4,117},{5,118},{6,119},{7,120},{8... | collective-permute-start | bytes 1572872 | tf_op jit(solution)/shard_map/ppermute | solution.py:498
  4.7 29.9 %collective-permute-start.2 = (bf16[2,512,512]{2,1,0:T(8,128)(2,1)S(1)}, bf16[2,512,512]{2,1,0:T(8,128)(2,1)S(1)}, u32[]{:S(2)}, u32[]{:S(2)}) collective-permute-start(bf16[2,512,512]{2,1,0:T(8,128)(2,1)S(1)} %pad_maximum_fusion), channel_id=1, source_target_pairs={{0,15},{1,0},{2,1},{3,2},{4,3},{5,4},{6,5},{7,6},{8,7},{9,8},{10,9... | collective-permute-start | bytes 3145736 | tf_op jit(solution)/shard_map/ppermute | solution.py:498
  19.9 10.8 %copy-start = (bf16[2,2,512,512]{3,2,1,0:T(8,128)(2,1)S(1)}, bf16[2,2,512,512]{3,2,1,0:T(8,128)(2,1)}, u32[]{:S(2)}) copy-start(bf16[2,2,512,512]{3,2,1,0:T(8,128)(2,1)} %h_ref.5) | copy-start | bytes 6291460
  19.9 10.8 %copy-start.1 = (bf16[2,2,512,512]{3,2,1,0:T(8,128)(2,1)S(1)}, bf16[2,2,512,512]{3,2,1,0:T(8,128)(2,1)}, u32[]{:S(2)}) copy-start(bf16[2,2,512,512]{3,2,1,0:T(8,128)(2,1)} %v_ref.5) | copy-start | bytes 6291460
  29.8 11.0 %collective-permute-start = (bf16[1040,128]{1,0:T(8,128)(2,1)S(1)}, bf16[1040,128]{1,0:T(8,128)(2,1)S(1)}, u32[]{:S(2)}, u32[]{:S(2)}) collective-permute-start(bf16[1040,128]{1,0:T(8,128)(2,1)S(1)} %get-tuple-element.49), channel_id=1, source_target_pairs={{0,15},{1,0},{2,1},{3,2},{4,3},{5,4},{6,5},{7,6},{8,7},{9,8},{10,9... | collective-permute-start | bytes 798728 | tf_op jit(solution)/shard_map/ppermute | solution.py:498
  32.2 12.0 %collective-permute-start.6 = (bf16[1040,128]{1,0:T(8,128)(2,1)S(1)}, bf16[1040,128]{1,0:T(8,128)(2,1)S(1)}, u32[]{:S(2)}, u32[]{:S(2)}) collective-permute-start(bf16[1040,128]{1,0:T(8,128)(2,1)S(1)} %get-tuple-element.54), channel_id=1, source_target_pairs={{0,16},{1,17},{2,18},{3,19},{4,20},{5,21},{6,22},{7,23},{8,24},{9,... | collective-permute-start | bytes 798728 | tf_op jit(solution)/shard_map/ppermute | solution.py:498
  34.6 39.0 %collective-permute-start.5 = (bf16[3088,128]{1,0:T(8,128)(2,1)S(1)}, bf16[3088,128]{1,0:T(8,128)(2,1)S(1)}, u32[]{:S(2)}, u32[]{:S(2)}) collective-permute-start(bf16[3088,128]{1,0:T(8,128)(2,1)S(1)} %get-tuple-element.53), channel_id=1, source_target_pairs={{0,1},{1,2},{2,3},{3,4},{4,5},{5,6},{6,7},{7,8},{8,9},{9,10},{10,1... | collective-permute-start | bytes 2371592 | tf_op jit(solution)/shard_map/ppermute | solution.py:498
  34.6 39.0 %collective-permute-start.3 = (bf16[2,512,512]{2,1,0:T(8,128)(2,1)S(1)}, bf16[2,512,512]{2,1,0:T(8,128)(2,1)S(1)}, u32[]{:S(2)}, u32[]{:S(2)}) collective-permute-start(bf16[2,512,512]{2,1,0:T(8,128)(2,1)S(1)} %collective-permute-done.2.rc), channel_id=1, source_target_pairs={{0,113},{1,114},{2,115},{3,116},{4,117},{5,118},{6,119},{7,120},{8... | collective-permute-start | bytes 3145736 | tf_op jit(solution)/shard_map/ppermute | solution.py:498
  40.8 32.8 %collective-permute-start.1 = (bf16[1040,128]{1,0:T(8,128)(2,1)S(1)}, bf16[1040,128]{1,0:T(8,128)(2,1)S(1)}, u32[]{:S(2)}, u32[]{:S(2)}) collective-permute-start(bf16[1040,128]{1,0:T(8,128)(2,1)S(1)} %collective-permute-done.rpack), channel_id=1, source_target_pairs={{0,113},{1,114},{2,115},{3,116},{4,117},{5,118},{6,119},{7,120},{8... | collective-permute-start | bytes 798728 | tf_op jit(solution)/shard_map/ppermute | solution.py:498
